TPU v7x, 128 devices: a whole 4x4x4 slice. The times are simulated.
128 devices in a mesh: leaf: 128 (over z, x, y, core).
Axes of the slice: x: 4, y: 4, z: 4, core: 2. Of those that a mesh axis runs over, the one named last changes fastest.
Arguments:
- coords: float32 [3, 1048576], P(None, 'leaf'), may hold values from 0 to 1
- charges: bfloat16 [1048576, 128], P('leaf'), may hold values from -6 to 6
- near_leaves: int32 [8192, 27], P('leaf'), may hold values from 0 to 191
- leaf_basis: bfloat16 [8192, 4096], P('leaf'), may hold values from -1 to 1
- leaf_transfer: bfloat16 [8192, 1024], P('leaf'), may hold values from -0.75 to 0.75
- mid_transfer: bfloat16 [1024, 1024], P('leaf'), may hold values from -0.75 to 0.75
- base_transfer: bfloat16 [128, 1024], P('leaf'), may hold values from -0.75 to 0.75
- base_coupling: bfloat16 [24192, 1024], P('leaf'), may hold values from -0.01953125 to 0.01953125
- base_target: int32 [24192, 1], P('leaf'), may hold values from 0 to 127; in each aligned block of 189 rows (0 to 188, 189 to 377, ...) at most 2 rows name the same one
- base_source: int32 [24192], P('leaf'), may hold values from 0 to 127
- top_coupling: bfloat16 [1024, 1024], P('leaf'), may hold values from -0.015625 to 0.015625
- top_target: int32 [1024], P('leaf'), may hold values from 0 to 15
- top_source: int32 [1024], P('leaf'), may hold values from 0 to 15
Outputs:
- potential: bfloat16 [1048576, 128], P('leaf')
Inputs may be any that keep to these rules, and one draw needn't show every extreme that they name: `near_leaves`: entry j of leaf l names leaf 64 * (l // 64 - 1) + j: a leaf of the device before in Morton order, of the row's own device, or of the device after; repeats may occur. `base_target`: among the 189 blocks of one device no base cluster is the target more than 2 times; that count is reached.
All inputs are finite; a program needn't handle non-finite values.
Results may differ from a plain program's by a relative error of at most 0.01.
Values may be sent and summed in bfloat16 or wider, within the bound.
A program may use at most 128 MiB of HBM per device.

v0:
```python
import math

import jax
import jax.numpy as jnp
from jax import lax
from jax.sharding import Mesh
from jax.sharding import PartitionSpec as P

K = 32
RHS = 128
M = 128
LEAF = ("leaf_0", "leaf_1", "leaf_2", "leaf_3")


delta_sq = 0.0025


def extended(array, sides, width):
    for axis, dim in sides:
        size, length = (lax.axis_size(axis), array.shape[dim])
        up = [(i, (i + 1) % size) for i in range(size - 1)]
        down = [(j, i) for i, j in up]
        last = lax.slice_in_dim(array, length - width, length, axis=dim)
        first = lax.slice_in_dim(array, 0, width, axis=dim)
        before = lax.ppermute(last, axis, up)
        after = lax.ppermute(first, axis, down)
        array = jnp.concatenate([before, array, after], axis=dim)
    return array


def in_one_piece(arrays, axis, dim, along):
    both = jnp.concatenate(arrays, axis=along)
    out, at, done = (lax.all_gather(both, axis, axis=dim, tiled=True), 0, [])
    for a in arrays:
        done.append(lax.slice_in_dim(out, at, at + a.shape[along], axis=along))
        at += a.shape[along]
    return tuple(done)


def rows_for(lines, length):
    spare = -len(lines) % length
    return jnp.pad(lines, [(0, spare)] + [(0, 0)] * (lines.ndim - 1))


def own_block(pieces, axes, order):
    lengths = [lax.axis_size(a) for a in axes]
    pieces = pieces.reshape(*lengths, *pieces.shape[1:])
    pieces = pieces.transpose(*order, *range(len(axes), pieces.ndim))
    pieces = pieces.reshape(-1, *pieces.shape[len(axes) :])
    for k in order:
        pieces = lax.psum_scatter(pieces, axes[k], scatter_dimension=0, tiled=True)
    return pieces[0]


def stacked_from(array, axes, order):
    pieces = array[None]
    for k in order:
        pieces = lax.all_gather(pieces, axes[k], axis=0, tiled=True)
    carried = [lax.axis_size(axes[k]) for k in reversed(order)]
    pieces = pieces.reshape(*carried, *array.shape)
    turned = sorted(range(len(order)), key=lambda place: order[len(order) - 1 - place])
    return pieces.transpose(*turned, *range(len(order), pieces.ndim)).reshape(-1, *array.shape)


def total_of(array, axes, order):
    length, lines = (lax.axis_size(axes), array.reshape(-1, *array.shape[1:][-1:]))
    pieces = rows_for(lines, length).reshape(length, -1, *lines.shape[1:])
    own = own_block(pieces, axes, order)
    whole = stacked_from(own, axes, order[::-1]).reshape(-1, *lines.shape[1:])
    return whole[: len(lines)].reshape(array.shape)


def in_blocks(array, dim, length):
    lengths = array.shape
    pieces = array.reshape(*lengths[:dim], length, lengths[dim] // length, *lengths[dim + 1 :])
    return jnp.moveaxis(pieces, dim, 0)


def scatter_pairs(array, chips, core, dim):
    sizes = (lax.axis_size(chips), lax.axis_size(core))
    pieces = in_blocks(array, dim, sizes[0] * sizes[1])
    inside = pieces.shape[1:]
    pieces = pieces.reshape(*sizes, *inside).swapaxes(0, 1).reshape(-1, *inside)
    pieces = lax.psum_scatter(pieces, core, scatter_dimension=0, tiled=True)
    return lax.psum_scatter(pieces, chips, scatter_dimension=0, tiled=True)[0]


def near_block(points, pool_points, pool_charges, columns):
    near_scale = 1.0 / math.sqrt(columns.shape[1] * points.shape[2])

    def near_step(running, column):
        other_points = jnp.take(pool_points, column, axis=1)
        other_charges = jnp.take(pool_charges, column, axis=0)
        squares = jnp.sum((points[:, :, :, None] - other_points[:, :, None, :]) ** 2, axis=0)
        kernel = (near_scale / jnp.sqrt(squares + delta_sq)).astype(jnp.bfloat16)
        update = jnp.einsum(
            "lab,lbr->lar", kernel, other_charges, preferred_element_type=jnp.float32
        )
        return (running + update, None)

    initial = jnp.zeros((points.shape[1], points.shape[2], pool_charges.shape[2]), jnp.float32)
    running, unused = lax.scan(near_step, initial, columns.T)
    return running


def per_device(
    coords,
    charges,
    near_leaves,
    leaf_basis,
    leaf_transfer,
    mid_transfer,
    base_transfer,
    base_coupling,
    base_target,
    base_source,
    top_coupling,
    top_target,
    top_source,
):
    single_precision = jnp.float32
    bf16 = jnp.bfloat16
    leaves = leaf_basis.shape[0]
    mid_count = leaves // 8
    base_count = leaves // 64
    devices = lax.axis_size(LEAF)
    position = lax.axis_index(LEAF)
    charge_row_block = charges.reshape(leaves, M, RHS)
    own_points = coords.reshape(3, leaves, M)
    point_rows = own_points.transpose(1, 0, 2).reshape(leaves, 3 * M)
    pool_points = (
        extended(point_rows, ((LEAF, 0),), leaves).reshape(3 * leaves, 3, M).transpose(1, 0, 2)
    )
    pool_charges = extended(
        charge_row_block.reshape(leaves, M * RHS), ((LEAF, 0),), leaves
    ).reshape(3 * leaves, M, RHS)
    basis_matrix = leaf_basis.reshape(leaves, K, M)
    leaf_coefficients = jnp.einsum(
        "xpt,xtu->xpu", basis_matrix, charge_row_block, preferred_element_type=single_precision
    ).astype(bf16)
    mid_coeffs = jnp.einsum(
        "mckp,mckr->mpr",
        leaf_transfer.reshape(mid_count, 8, K, K),
        leaf_coefficients.reshape(mid_count, 8, K, RHS),
        preferred_element_type=single_precision,
    ).astype(bf16)
    base_coeffs = jnp.einsum(
        "mckp,mckr->mpr",
        mid_transfer.reshape(base_count, 8, K, K),
        mid_coeffs.reshape(base_count, 8, K, RHS),
        preferred_element_type=single_precision,
    ).astype(bf16)
    base_lift = base_transfer.reshape(base_count, K, K)
    lifted = jnp.einsum(
        "bkp,bkr->bpr", base_lift, base_coeffs, preferred_element_type=single_precision
    ).astype(bf16)
    all_coeffs, all_lifted = in_one_piece(
        (base_coeffs.reshape(base_count, K * RHS), lifted.reshape(base_count, K * RHS)), LEAF, 0, 1
    )
    total_bases = base_count * devices
    total_tops = total_bases // 8
    every_base = all_coeffs.reshape(total_bases, K, RHS)
    top_coeffs = jnp.sum(
        all_lifted.reshape(total_tops, 8, K, RHS).astype(single_precision), axis=1
    ).astype(bf16)
    top_products = jnp.einsum(
        "bts,bsr->btr",
        top_coupling.reshape(-1, K, K),
        jnp.take(top_coeffs, top_source, axis=0),
        preferred_element_type=single_precision,
    )
    top_partial = jax.ops.segment_sum(top_products, top_target, num_segments=total_tops)
    top_sum = total_of(top_partial, LEAF, (0, 1, 2, 3))
    top_field = top_sum.astype(bf16)
    targets = base_target[:, 0]
    sources = jnp.take(every_base, base_source, axis=0)
    products = jnp.einsum(
        "bts,bsr->btr",
        base_coupling.reshape(-1, K, K),
        sources,
        preferred_element_type=single_precision,
    ).reshape(-1, K * RHS)
    first_row = jnp.int32(0)
    inside = (targets >= first_row) & (
        targets
        < first_row
        + base_count * lax.axis_size(("leaf_0", "leaf_1", "leaf_2")) * lax.axis_size("leaf_3")
    )
    labels = jnp.where(
        inside,
        targets,
        base_count * lax.axis_size(("leaf_0", "leaf_1", "leaf_2")) * lax.axis_size("leaf_3"),
    )
    coupled = scatter_pairs(
        jax.ops.segment_sum(
            products,
            labels,
            num_segments=base_count
            * lax.axis_size(("leaf_0", "leaf_1", "leaf_2"))
            * lax.axis_size("leaf_3"),
        ),
        ("leaf_0", "leaf_1", "leaf_2"),
        "leaf_3",
        0,
    ).reshape(base_count, K, RHS)
    my_bases = position * base_count + jnp.arange(base_count, dtype=jnp.int32)
    top_mine = jnp.take(top_field, my_bases // 8, axis=0)
    base_field = (
        coupled
        + jnp.einsum("bkp,bpr->bkr", base_lift, top_mine, preferred_element_type=single_precision)
    ).astype(bf16)
    mid_field = jnp.einsum(
        "mkp,mpr->mkr",
        mid_transfer.reshape(mid_count, K, K),
        jnp.repeat(base_field, 8, axis=0),
        preferred_element_type=single_precision,
    ).astype(bf16)
    leaf_potential = jnp.einsum(
        "lkp,lpr->lkr",
        leaf_transfer.reshape(leaves, K, K),
        jnp.repeat(mid_field, 8, axis=0),
        preferred_element_type=single_precision,
    ).astype(bf16)
    near_field = near_block(own_points, pool_points, pool_charges, near_leaves)
    distant_field = jnp.einsum(
        "cbz,cbw->czw", basis_matrix, leaf_potential, preferred_element_type=single_precision
    )
    return (near_field + distant_field).astype(bf16).reshape(leaves * M, RHS)


def solution(mesh):
    split = Mesh(mesh.devices.reshape(4, 4, 4, 2), ("leaf_0", "leaf_1", "leaf_2", "leaf_3"))
    in_specs = (
        P(None, LEAF),
        P(LEAF, None),
        P(LEAF, None),
        P(LEAF, None),
        P(LEAF, None),
        P(LEAF, None),
        P(LEAF, None),
        P(LEAF, None),
        P(LEAF, None),
        P(LEAF),
        P(LEAF, None),
        P(LEAF),
        P(LEAF),
    )
    out_specs = P(LEAF, None)
    return jax.shard_map(
        per_device, mesh=split, in_specs=in_specs, out_specs=out_specs, check_vma=False
    )
```

profile of v0, /device:TPU:32, one launch (start us, length us, event | category | flops | bytes accessed | tf_op | source)
XLA Modules:
  0.0 743.9 jit_solution(6363721647622116854)
XLA Ops:
  16.4 65.0 %all-gather.3.cloned.1.call-done = bf16[128,1,8192]{2,1,0:T(2,128)(2,1)} async-done(((bf16[1,1,8192]{2,1,0:T(2,128)(2,1)}), bf16[128,1,8192]{2,1,0:T(2,128)(2,1)}) %all-gather.3.cloned.1.call-update) | async-done | bytes 2097168 | tf_op jit(solution)/shard_map/all_gather | solution.py:33
  98.2 6.3 scatter_custom_fusion
  122.7 7.9 %collective-permute-start.1 = (f32[64,384]{1,0:T(8,128)S(1)}, f32[64,384]{1,0:T(8,128)S(1)}, u32[]{:S(2)}, u32[]{:S(2)}) collective-permute-start(f32[64,384]{1,0:T(8,128)S(1)} %bitcast.168), channel_id=1, source_target_pairs={{1,0},{2,1},{3,2},{4,3},{5,4},{6,5},{7,6},{8,7},{9,8},{10,9},{11,1... | collective-permute-start | bytes 294920 | tf_op jit(solution)/shard_map/ppermute | solution.py:26
  145.6 8.0 %collective-permute-done = f32[64,384]{1,0:T(8,128)S(1)} collective-permute-done((f32[64,384]{1,0:T(8,128)S(1)}, f32[64,384]{1,0:T(8,128)S(1)}, u32[]{:S(2)}, u32[]{:S(2)}) %collective-permute-start) | collective-permute-done | bytes 98336 | tf_op jit(solution)/shard_map/ppermute | solution.py:25
  167.9 505.8 %while.12 = (s32[]{:T(128)}, f32[64,128,128]{2,1,0:T(8,128)}, f32[3,8192]{1,0:T(4,128)S(1)}, s32[27,64]{1,0:T(8,128)}, f32[3,192,128]{2,0,1:T(4,128)S(1)}, /*ind...) while((s32[]{:T(128)}, f32[64,128,128]{2,1,0:T(8,128)}, f32[3,8192]{1,0:T(4,128)S(1)}, ...), condition=%wide.region_2.3_spmd.clone, body=%wide.region_0.2_spmd.clone.sunk | while | flops 283141696 | bytes 24057648 | solution.py:102
  170.2 6.2 multiply_reduce_fusion.2
  187.7 6.2 multiply_reduce_fusion.2
  197.6 6.6 select_add_fusion.2
  206.5 6.2 multiply_reduce_fusion.2
  216.4 6.6 select_add_fusion.2
  225.2 6.2 multiply_reduce_fusion.2
  235.2 6.6 select_add_fusion.2
  254.0 6.6 select_add_fusion.2
  272.8 6.6 select_add_fusion.2
  281.6 6.2 multiply_reduce_fusion.2
  291.6 6.6 select_add_fusion.2
  310.4 6.6 select_add_fusion.2
  329.2 6.7 select_add_fusion.2
  348.1 6.6 select_add_fusion.2
  366.9 6.6 select_add_fusion.2
  385.7 6.6 select_add_fusion.2
  404.4 6.6 select_add_fusion.2
  413.3 6.2 multiply_reduce_fusion.2
  423.2 6.6 select_add_fusion.2
  432.0 6.2 multiply_reduce_fusion.2
  442.0 6.6 select_add_fusion.2
  460.7 6.6 select_add_fusion.2
  479.5 6.6 select_add_fusion.2
  488.3 6.2 multiply_reduce_fusion.2
  498.3 6.6 select_add_fusion.2
  507.1 6.2 multiply_reduce_fusion.2
  517.0 6.6 select_add_fusion.2
  535.8 6.6 select_add_fusion.2
  554.6 6.6 select_add_fusion.2
  573.3 6.6 select_add_fusion.2
  582.1 6.2 multiply_reduce_fusion.2
  592.1 6.6 select_add_fusion.2
  610.9 6.6 select_add_fusion.2
  619.7 6.2 multiply_reduce_fusion.2
  629.6 6.6 select_add_fusion.2
  638.4 6.2 multiply_reduce_fusion.2
  648.4 6.6 select_add_fusion.2
  657.2 6.2 multiply_reduce_fusion.2
  667.2 6.6 select_add_fusion.2
  674.4 16.7 %all-reduce.3 = f32[8,4,128]{2,1,0:T(4,128)S(1)} all-reduce(f32[8,4,128]{2,1,0:T(4,128)S(1)} %constant_dynamic-slice_fusion.3), channel_id=6, replica_groups=mesh['leaf_0'=4,'leaf_1'=4,'leaf_2'=4,'leaf_3'=2] {'leaf_2'}, use_global_device_ids=true, to_apply=%region_10.11.clone | all-reduce | flops 4096 | bytes 32768
  696.0 10.4 %all_gather.17 = bf16[8,4,128]{2,1,0:T(4,128)(2,1)S(1)} all-gather(bf16[2,4,128]{2,1,0:T(4,128)(2,1)S(1)} %all_gather.16), channel_id=1, replica_groups=mesh['leaf_0'=4,'leaf_1'=4,'leaf_2'=4,'leaf_3'=2] {'leaf_2'}, dimensions={0}, use_global_device_ids=true | all-gather | bytes 10240 | tf_op jit(solution)/shard_map/all_gather | solution.py:58
  706.5 12.4 %all_gather.18 = bf16[32,4,128]{2,1,0:T(4,128)(2,1)S(1)} all-gather(bf16[8,4,128]{2,1,0:T(4,128)(2,1)S(1)} %all_gather.17), channel_id=1, replica_groups=mesh['leaf_0'=4,'leaf_1'=4,'leaf_2'=4,'leaf_3'=2] {'leaf_1'}, dimensions={0}, use_global_device_ids=true | all-gather | bytes 40960 | tf_op jit(solution)/shard_map/all_gather | solution.py:58
  718.8 12.1 %all_gather.19 = bf16[128,4,128]{2,1,0:T(4,128)(2,1)S(1)} all-gather(bf16[32,4,128]{2,1,0:T(4,128)(2,1)S(1)} %all_gather.18), channel_id=1, replica_groups=mesh['leaf_0'=4,'leaf_1'=4,'leaf_2'=4,'leaf_3'=2] {'leaf_0'}, dimensions={0}, use_global_device_ids=true | all-gather | bytes 163840 | tf_op jit(solution)/shard_map/all_gather | solution.py:58
  (346 shorter events, 336.7 us)
Async XLA Ops:
  6.5 74.9 %all-gather.3.cloned.1.call-start = ((), (), s32[]{:S(2)}) async-start(), calls=%async_computation.2 | async-start | bytes 4227072 | tf_op jit(solution)/shard_map/all_gather | solution.py:33
  8.5 4.9 copy-start.3
  10.7 3.7 copy-start.6
  12.9 3.2 copy-start.7
  13.0 3.3 copy-start.8
  13.0 3.4 copy-start.11
  13.0 3.4 copy-start.9
  14.3 146.4 %all-reduce.11.cloned.1.call-start = ((), (), s32[]{:S(2)}) async-start(), calls=%async_computation.4 | async-start | bytes 524288
  85.9 1.8 copy-start.10
  88.5 0.7 copy-start.2
  89.3 78.6 %reduce-scatter.3.cloned.1.call-start = ((), (), s32[]{:S(2)}) async-start(), calls=%async_computation.1 | async-start | bytes 3145728 | tf_op jit(solution)/shard_map/reduce_scatter | solution.py:84
  110.9 1.6 copy-start
  110.9 11.8 %copy-start.1 = (f32[3,8192]{1,0:T(4,128)S(1)}, f32[3,8192]{1,0:T(4,128)}, u32[]{:S(2)}) copy-start(f32[3,8192]{1,0:T(4,128)} %param.15) | copy-start | bytes 294916
  110.9 21.8 %copy-start.5 = (bf16[64,1024]{1,0:T(8,128)(2,1)S(1)}, bf16[64,1024]{1,0:T(8,128)(2,1)}, u32[]{:S(2)}) copy-start(bf16[64,1024]{1,0:T(8,128)(2,1)} %param.19) | copy-start | bytes 393220
  110.9 23.5 %copy-start.16 = (u32[128]{0:T(128)S(1)}, u32[128]{0:T(128)}, u32[]{:S(2)}) copy-start(u32[128]{0:T(128)} %constant.173) | copy-start | bytes 1540
  111.0 24.2 %copy-start.15 = (u32[128]{0:T(128)S(1)}, u32[128]{0:T(128)}, u32[]{:S(2)}) copy-start(u32[128]{0:T(128)} %constant.177) | copy-start | bytes 1540
  111.0 24.8 %copy-start.14 = (u32[128]{0:T(128)S(1)}, u32[128]{0:T(128)}, u32[]{:S(2)}) copy-start(u32[128]{0:T(128)} %constant.181) | copy-start | bytes 1540
  111.0 25.3 %copy-start.13 = (u32[128]{0:T(128)S(1)}, u32[128]{0:T(128)}, u32[]{:S(2)}) copy-start(u32[128]{0:T(128)} %constant.185) | copy-start | bytes 1540
  111.0 25.9 %copy-start.12 = (u32[128]{0:T(128)S(1)}, u32[128]{0:T(128)}, u32[]{:S(2)}) copy-start(u32[128]{0:T(128)} %constant.189) | copy-start | bytes 1540
  111.0 562.7 %all-reduce.13.cloned.1.call-start = ((), (), s32[]{:S(2)}) async-start(), calls=%async_computation.5 | async-start | bytes 131072
  114.8 39.0 %collective-permute-start.3 = (bf16[64,16384]{1,0:T(8,128)(2,1)}, bf16[64,16384]{1,0:T(8,128)(2,1)}, u32[]{:S(2)}, u32[]{:S(2)}) collective-permute-start(bf16[64,16384]{1,0:T(8,128)(2,1)} %reshape_reshape.6), channel_id=1, source_target_pairs={{1,0},{2,1},{3,2},{4,3},{5,4},{6,5},{7,6},{8,7},{9,8},{10,9},{11,1... | collective-permute-start | bytes 6291464 | tf_op jit(solution)/shard_map/ppermute | solution.py:26
  120.8 36.5 %collective-permute-start.2 = (bf16[64,16384]{1,0:T(8,128)(2,1)}, bf16[64,16384]{1,0:T(8,128)(2,1)}, u32[]{:S(2)}, u32[]{:S(2)}) collective-permute-start(bf16[64,16384]{1,0:T(8,128)(2,1)} %reshape_reshape.6), channel_id=1, source_target_pairs={{0,1},{1,2},{2,3},{3,4},{4,5},{5,6},{6,7},{7,8},{8,9},{9,10},{10,1... | collective-permute-start | bytes 6291464 | tf_op jit(solution)/shard_map/ppermute | solution.py:25
  122.7 22.8 %collective-permute-start.1 = (f32[64,384]{1,0:T(8,128)S(1)}, f32[64,384]{1,0:T(8,128)S(1)}, u32[]{:S(2)}, u32[]{:S(2)}) collective-permute-start(f32[64,384]{1,0:T(8,128)S(1)} %bitcast.168), channel_id=1, source_target_pairs={{1,0},{2,1},{3,2},{4,3},{5,4},{6,5},{7,6},{8,7},{9,8},{10,9},{11,1... | collective-permute-start | bytes 294920 | tf_op jit(solution)/shard_map/ppermute | solution.py:26
  130.6 23.0 %collective-permute-start = (f32[64,384]{1,0:T(8,128)S(1)}, f32[64,384]{1,0:T(8,128)S(1)}, u32[]{:S(2)}, u32[]{:S(2)}) collective-permute-start(f32[64,384]{1,0:T(8,128)S(1)} %bitcast.169), channel_id=1, source_target_pairs={{0,1},{1,2},{2,3},{3,4},{4,5},{5,6},{6,7},{7,8},{8,9},{9,10},{10,1... | collective-permute-start | bytes 294920 | tf_op jit(solution)/shard_map/ppermute | solution.py:25
  162.2 568.7 %all-reduce.9.cloned.1.call-start = ((), (), s32[]{:S(2)}) async-start(), calls=%async_computation.3 | async-start | bytes 2097152
  167.9 564.8 %copy-start.4 = (bf16[8,32,32]{2,1,0:T(8,128)(2,1)S(1)}, bf16[8,32,32]{2,1,0:T(8,128)(2,1)}, u32[]{:S(2)}) copy-start(bf16[8,32,32]{2,1,0:T(8,128)(2,1)} %copy-done.3) | copy-start | bytes 49156
Sparse Core Ops, SparseCore 0:
  14.4 66.8 all-gather.2
  89.4 40.1 all-reduce.10
  131.9 35.7 reduce-scatter.2
  169.8 42.3 all-reduce.12
  216.9 129.5 all-reduce.8
where the time goes:
time: 748 us; the launch traced here: 744 us
  other arithmetic  224 us (30%)
  matrix products  186 us (25%)
  local copies, waits for them, and re-layouts  163 us (22%)
  waiting for transfers between devices  79.2 us (11%)
  blocking collectives  55.9 us (7%)
  starting transfers between devices  18.3 us (2%)
  between operations  15.5 us (2%)
    dot_general x27, matrix products, near_step(): jnp.einsum('lab,lbr->lar', kernel, other_charges, preferred_element_type=...  177 us
    reduce_sum x27, other arithmetic, near_step(): jnp.sum((points[:, :, :, None] - other_points[:, :, None, :]) ** 2, axis=0)  168 us
    gather x27, local copies, waits for them, and re-layouts, near_step(): other_charges = jnp.take(pool_charges, column, axis=0)  101 us
    all_gather x1, waiting for transfers between devices, in_one_piece(): out, at, done = (lax.all_gather(both, axis, axis=dim, tiled=True), 0, [])  65 us
    all_gather x4, blocking collectives, stacked_from(): pieces = lax.all_gather(pieces, axes[k], axis=0, tiled=True)  36.7 us
    unnamed x55, local copies, waits for them, and re-layouts  27.6 us
    select_n x54, other arithmetic, near_step(): other_points = jnp.take(pool_points, column, axis=1)  22.4 us
    unnamed x2, blocking collectives  19.1 us
  transfers between devices with their start and end apart: 9, of which 3 were waited for; matrix products, arithmetic and copies ran while one was open for 74% of the time, Pallas kernels for 0%

commit v1 on v0

v1 whole, which is shorter than its diff:
```python
import functools
import math

import jax
import jax.numpy as jnp
from jax import lax
from jax.experimental import pallas as pl
from jax.experimental.pallas import tpu as pltpu
from jax.sharding import PartitionSpec as P

K = 32
RHS = 128
M = 128
N = 128
LEAVES = 64
POOL = 3 * LEAVES
NNEAR = 27
PAIRS = (NNEAR + 1) // 2
GROUP = 8
DELTA_SQ = 0.0025
AXIS = "leaf"
MESH = pl.DeviceIdType.MESH
bf16 = jnp.bfloat16
f32 = jnp.float32


def dot(a, b):
    return jnp.dot(a, b, preferred_element_type=f32)


def dot_t(a, b):
    return lax.dot_general(a, b, (((0,), (0,)), ((), ())), preferred_element_type=f32)


def vmem(*shape):
    return pl.BlockSpec(shape, lambda *_: (0,) * len(shape))


def split3(v):
    high = v.astype(bf16).astype(f32)
    rest = v - high
    mid = rest.astype(bf16).astype(f32)
    return high, mid, rest - mid


def features(scale, points, target):
    centred = [(p - 0.5) * scale for p in points]
    norm = centred[0] * centred[0] + centred[1] * centred[1] + centred[2] * centred[2]
    one = jnp.ones_like(norm)
    rows = []
    for c in centred:
        h, m, l = split3(c)
        if target:
            h, m, l = -2.0 * h, -2.0 * m, -2.0 * l
            rows += [h, h, m, m, h, l]
        else:
            rows += [h, m, h, m, l, h]
    if target:
        rows += [*split3(norm + scale * scale * DELTA_SQ), one, one, one]
    else:
        rows += [one, one, one, *split3(norm)]
    return rows + [jnp.zeros_like(norm)] * (K - len(rows))


def feature_kernel(scale, points, source, target, lines):
    count = points.shape[1]
    for r, row in enumerate(features(scale, [points[i] for i in range(3)], False)):
        lines[pl.ds(r, count, stride=K), :] = row

    def put(l, c):
        source[l] = lines[pl.ds(pl.multiple_of(l * K, K), K), :].astype(bf16)
        return c

    lax.fori_loop(0, count, put, 0, unroll=4)
    own = [points[i, LEAVES : 2 * LEAVES] for i in range(3)]
    for r, row in enumerate(features(scale, own, True)):
        lines[pl.ds(r, LEAVES, stride=K), :] = row

    def turn(l, c):
        target[l] = lines[pl.ds(pl.multiple_of(l * K, K), K), :].T.astype(bf16)
        return c

    lax.fori_loop(0, LEAVES, turn, 0, unroll=4)


def feature_call(points):
    count = points.shape[1]
    return pl.pallas_call(
        functools.partial(feature_kernel, math.sqrt(NNEAR * M)),
        out_shape=(
            jax.ShapeDtypeStruct((count, K, M), bf16),
            jax.ShapeDtypeStruct((LEAVES, M, K), bf16),
        ),
        scratch_shapes=[pltpu.VMEM((count * K, M), f32)],
        cost_estimate=pl.CostEstimate(flops=10**8, bytes_accessed=10**6, transcendentals=0),
        name="features",
    )(points)


def upward_kernel(charges, basis, leaf_t, mid_t, base_t, out, mids):
    step = pl.program_id(0)
    parts = []
    for c in range(GROUP):
        parts.append(dot(basis[c], charges[c]).astype(bf16))
    rows = jnp.concatenate(parts, axis=0)
    mids[pl.ds(pl.multiple_of(step * K, K), K), :] = dot_t(leaf_t[...], rows).astype(bf16)

    @pl.when(step == GROUP - 1)
    def _():
        base = dot_t(mid_t[...], mids[...]).astype(bf16)
        out[0] = base
        out[1] = dot_t(base_t[...], base).astype(bf16)


def upward_call(charges, basis, leaf_t, mid_t, base_t):
    return pl.pallas_call(
        upward_kernel,
        grid=(GROUP,),
        in_specs=[
            pl.BlockSpec((GROUP, M, RHS), lambda i: (i, 0, 0)),
            pl.BlockSpec((GROUP, K, M), lambda i: (i, 0, 0)),
            pl.BlockSpec((GROUP * K, K), lambda i: (i, 0)),
            vmem(GROUP * K, K),
            vmem(K, K),
        ],
        out_specs=vmem(2, K, RHS),
        out_shape=jax.ShapeDtypeStruct((2, K, RHS), bf16),
        scratch_shapes=[pltpu.VMEM((GROUP * K, RHS), bf16)],
        cost_estimate=pl.CostEstimate(flops=10**8, bytes_accessed=3 * 10**6, transcendentals=0),
        name="upward",
    )(charges, basis, leaf_t, mid_t, base_t)


def blocks_kernel(blk, blk_src, top, top_idx, r_blk, r_src, r_top, r_idx, send, recv, local):
    me = lax.axis_index(AXIS)
    plane, place = me // GROUP, me % GROUP
    barrier = pltpu.get_barrier_semaphore()

    def hello(o, c):
        pl.semaphore_signal(
            barrier, inc=1, device_id=(lax.rem(me + o, N),), device_id_type=MESH
        )
        return c

    lax.fori_loop(1, N, hello, 0)
    pl.semaphore_wait(barrier, N - 1)

    def remote(src, dst, k, to):
        return pltpu.make_async_remote_copy(
            src_ref=src,
            dst_ref=dst,
            send_sem=send.at[k],
            recv_sem=recv.at[k],
            device_id=(to,),
            device_id_type=MESH,
        )

    def give(o, c):
        to = lax.rem(me + o, N)
        remote(blk.at[to], r_blk.at[me], 0, to).start()
        remote(blk_src.at[to], r_src.at[me], 1, to).start()
        return c

    lax.fori_loop(1, N, give, 0)

    def give_top(o, c):
        to = lax.rem(plane + o, 16) * GROUP + place
        remote(top, r_top.at[plane], 2, to).start()
        remote(top_idx, r_idx.at[plane], 3, to).start()
        return c

    lax.fori_loop(1, 16, give_top, 0)
    own = [
        pltpu.make_async_copy(blk.at[me], r_blk.at[me], local.at[0]),
        pltpu.make_async_copy(blk_src.at[me], r_src.at[me], local.at[1]),
        pltpu.make_async_copy(top, r_top.at[plane], local.at[2]),
        pltpu.make_async_copy(top_idx, r_idx.at[plane], local.at[3]),
    ]
    for copy in own:
        copy.start()
    for copy in own:
        copy.wait()
    for k, (ref, count) in enumerate(((r_blk, N), (r_src, N), (r_top, 16), (r_idx, 16))):
        part = ref.at[pl.ds(0, count - 1)]
        whole = remote(part, part, k, me)
        whole.wait_send()
        whole.wait_recv()


def blocks_call(blk, blk_src, top, top_idx):
    return pl.pallas_call(
        blocks_kernel,
        out_shape=(
            jax.ShapeDtypeStruct(blk.shape, blk.dtype),
            jax.ShapeDtypeStruct(blk_src.shape, blk_src.dtype),
            jax.ShapeDtypeStruct((16, *top.shape), top.dtype),
            jax.ShapeDtypeStruct((16, *top_idx.shape), top_idx.dtype),
        ),
        in_specs=[pl.BlockSpec(memory_space=pltpu.VMEM)] * 4,
        out_specs=(pl.BlockSpec(memory_space=pltpu.VMEM),) * 4,
        scratch_shapes=[
            pltpu.SemaphoreType.DMA((4,)),
            pltpu.SemaphoreType.DMA((4,)),
            pltpu.SemaphoreType.DMA((4,)),
        ],
        compiler_params=pltpu.CompilerParams(collective_id=0, has_side_effects=True),
        cost_estimate=pl.CostEstimate(flops=10**8, bytes_accessed=10**6, transcendentals=0),
        name="blocks",
    )(blk, blk_src, top, top_idx)


def field_kernel(
    coeffs, top_part, a_high, a_low, base_t, out, every, lifted, tops, mine, top_all, send, recv, local
):
    me = lax.axis_index(AXIS)
    plane, place = me // GROUP, me % GROUP
    core, y = place % 2, place // 2
    barrier = pltpu.get_barrier_semaphore()
    for o in range(1, GROUP):
        to = plane * GROUP + lax.rem(place + o, GROUP)
        pl.semaphore_signal(barrier, inc=1, device_id=(to,), device_id_type=MESH)
    for o in range(1, 16):
        to = lax.rem(plane + o, 16) * GROUP + place
        pl.semaphore_signal(barrier, inc=1, device_id=(to,), device_id_type=MESH)
    pl.semaphore_wait(barrier, GROUP + 14)

    def remote(src, dst, k, to):
        return pltpu.make_async_remote_copy(
            src_ref=src,
            dst_ref=dst,
            send_sem=send.at[k],
            recv_sem=recv.at[k],
            device_id=(to,),
            device_id_type=MESH,
        )

    def finish(part, k):
        whole = remote(part, part, k, me)
        whole.wait_send()
        whole.wait_recv()

    for o in range(1, 4):
        to = plane * GROUP + lax.rem(y + o, 4) * 2 + core
        remote(coeffs.at[0], every.at[core, plane, y], 0, to).start()
    for o in range(1, GROUP):
        to = plane * GROUP + lax.rem(place + o, GROUP)
        remote(coeffs.at[1], lifted.at[place], 1, to).start()
    for o in range(1, GROUP):
        to = plane * GROUP + lax.rem(place + o, GROUP)
        remote(top_part, tops.at[place], 2, to).start()
    own = [
        pltpu.make_async_copy(coeffs.at[0], every.at[core, plane, y], local.at[0]),
        pltpu.make_async_copy(coeffs.at[1], lifted.at[place], local.at[1]),
        pltpu.make_async_copy(top_part, tops.at[place], local.at[2]),
    ]
    for copy in own:
        copy.start()
    for copy in own:
        copy.wait()
    finish(lifted.at[pl.ds(0, 3)], 0)
    for o in range(1, 16):
        to = lax.rem(plane + o, 16) * GROUP + place
        remote(every.at[core, plane], every.at[core, plane], 3, to).start()
    finish(lifted.at[pl.ds(0, GROUP - 1)], 1)
    mine[...] = jnp.sum(lifted[...].astype(f32), axis=0).astype(bf16)
    for o in range(1, 16):
        to = lax.rem(plane + o, 16) * GROUP + place
        remote(mine, top_all.at[plane], 4, to).start()
    own_top = pltpu.make_async_copy(mine, top_all.at[plane], local.at[3])
    own_top.start()
    own_top.wait()
    finish(every.at[0, pl.ds(0, 15)], 3)
    partner = me + 1 - 2 * core
    across = remote(every.at[core], every.at[core], 5, partner)
    across.start()
    finish(tops.at[pl.ds(0, GROUP - 1)], 2)
    finish(top_all.at[pl.ds(0, 15)], 4)
    top = jnp.sum(tops[...].astype(f32), axis=0)
    top_high = top.astype(bf16)
    top_low = (top - top_high.astype(f32)).astype(bf16)
    coeff_tops = top_all[...].reshape(16 * K, RHS)
    top_field = (dot(top_high, coeff_tops) + dot(top_low, coeff_tops)).astype(bf16)
    total = dot(base_t[...], top_field)
    across.wait()
    rows = every[...].reshape(N * K, RHS)
    total = total + (dot(a_high[...], rows) + dot(a_low[...], rows))
    out[...] = total.astype(bf16)


def field_call(coeffs, top_part, a_high, a_low, base_t):
    return pl.pallas_call(
        field_kernel,
        out_shape=jax.ShapeDtypeStruct((K, RHS), bf16),
        in_specs=[pl.BlockSpec(memory_space=pltpu.VMEM)] * 5,
        out_specs=pl.BlockSpec(memory_space=pltpu.VMEM),
        scratch_shapes=[
            pltpu.VMEM((2, 16, 4, K, RHS), bf16),
            pltpu.VMEM((GROUP, K, RHS), bf16),
            pltpu.VMEM((GROUP, K, 16 * K), bf16),
            pltpu.VMEM((K, RHS), bf16),
            pltpu.VMEM((16, K, RHS), bf16),
            pltpu.SemaphoreType.DMA((6,)),
            pltpu.SemaphoreType.DMA((6,)),
            pltpu.SemaphoreType.DMA((4,)),
        ],
        compiler_params=pltpu.CompilerParams(collective_id=1, has_side_effects=True),
        cost_estimate=pl.CostEstimate(flops=10**8, bytes_accessed=10**6, transcendentals=0),
        name="field",
    )(coeffs, top_part, a_high, a_low, base_t)


def near_kernel(
    near, source, target, before, here, after, base, mid_t, leaf_t, basis, out, pool, kern, gathered, sems
):
    step = pl.program_id(0)

    @pl.when(step == 0)
    def _():
        copies = [
            pltpu.make_async_copy(ref, pool.at[pl.ds(LEAVES * i, LEAVES)], sems.at[i])
            for i, ref in enumerate((before, here, after))
        ]
        for copy in copies:
            copy.start()
        pool[POOL] = jnp.zeros((M, RHS), bf16)
        for copy in copies:
            copy.wait()

    mid = dot(mid_t[...], base[...]).astype(bf16)
    fields = dot(leaf_t[...], mid).astype(bf16)
    for b in range(GROUP):
        leaf = step * GROUP + b
        mine = target[b]
        for j in range(PAIRS):
            one = near[leaf * 2 * PAIRS + 2 * j]
            two = near[leaf * 2 * PAIRS + 2 * j + 1]
            others = jnp.concatenate([source[one], source[two]], axis=1)
            squares = dot(mine, others)
            kern[b, :, 2 * M * j : 2 * M * (j + 1)] = lax.rsqrt(squares.astype(bf16))
            gathered[b, 2 * M * j : 2 * M * j + M] = pool[one]
            gathered[b, 2 * M * j + M : 2 * M * (j + 1)] = pool[two]
        far = dot_t(basis[b], fields[b * K : (b + 1) * K])
        total = dot(kern[b], gathered[b]) + far
        out[pl.ds(b * M, M), :] = total.astype(bf16)


def near_call(near, source, target, before, here, after, base, mid_t, leaf_t, basis):
    count = source.shape[0]
    grid_spec = pltpu.PrefetchScalarGridSpec(
        num_scalar_prefetch=1,
        grid=(LEAVES // GROUP,),
        in_specs=[
            vmem(count, K, M),
            pl.BlockSpec((GROUP, M, K), lambda i, _: (i, 0, 0)),
            pl.BlockSpec(memory_space=pl.ANY),
            pl.BlockSpec(memory_space=pl.ANY),
            pl.BlockSpec(memory_space=pl.ANY),
            vmem(K, RHS),
            pl.BlockSpec((K, K), lambda i, _: (i, 0)),
            pl.BlockSpec((GROUP * K, K), lambda i, _: (i, 0)),
            pl.BlockSpec((GROUP, K, M), lambda i, _: (i, 0, 0)),
        ],
        out_specs=pl.BlockSpec((GROUP * M, RHS), lambda i, _: (i, 0)),
        scratch_shapes=[
            pltpu.VMEM((POOL + 1, M, RHS), bf16),
            pltpu.VMEM((GROUP, M, 2 * M * PAIRS), bf16),
            pltpu.VMEM((GROUP, 2 * M * PAIRS, RHS), bf16),
            pltpu.SemaphoreType.DMA((3,)),
        ],
    )
    return pl.pallas_call(
        near_kernel,
        grid_spec=grid_spec,
        out_shape=jax.ShapeDtypeStruct((LEAVES * M, RHS), bf16),
        compiler_params=pltpu.CompilerParams(
            vmem_limit_bytes=48 * 1024 * 1024, dimension_semantics=("arbitrary",)
        ),
        cost_estimate=pl.CostEstimate(
            flops=10**10, bytes_accessed=10**7, transcendentals=3 * 10**7
        ),
        name="near",
    )(near, source, target, before, here, after, base, mid_t, leaf_t, basis)


def high_low(v):
    high = v.astype(bf16)
    return high, (v - high.astype(f32)).astype(bf16)


def per_device(
    coords,
    charges,
    near_leaves,
    leaf_basis,
    leaf_transfer,
    mid_transfer,
    base_transfer,
    base_coupling,
    base_target,
    base_source,
    top_coupling,
    top_target,
    top_source,
):
    me = lax.axis_index(AXIS)
    up = [(i, i + 1) for i in range(N - 1)]
    down = [(i + 1, i) for i in range(N - 1)]
    rows = charges.reshape(LEAVES, M, RHS)
    before = lax.ppermute(rows, AXIS, up)
    after = lax.ppermute(rows, AXIS, down)
    points = coords.reshape(3, LEAVES, M)
    points = jnp.concatenate(
        [
            lax.ppermute(points, AXIS, up),
            points,
            lax.ppermute(points, AXIS, down),
            jnp.zeros((3, 8, M), f32),
        ],
        axis=1,
    )
    source, target = feature_call(points)

    targets = base_target[:, 0]
    count = targets.shape[0]
    earlier = jnp.arange(count)[:, None] > jnp.arange(count)[None, :]
    rank = jnp.sum((targets[:, None] == targets[None, :]) & earlier, axis=1)
    slots = jnp.arange(2 * N)
    chosen = (slots[:, None] == (2 * targets + rank)[None, :]).astype(bf16)
    blk = dot(chosen, base_coupling).astype(bf16).reshape(N, 16, 128)
    order = (base_source % 2) * 64 + (base_source // 8) * 4 + (base_source // 2) % 4
    slot_source = jnp.sum(chosen.astype(jnp.int32) * (order + 1)[None, :], axis=1) - 1
    blk_src = jnp.pad(slot_source.reshape(N, 1, 2), ((0, 0), (0, 0), (0, 126)))
    top_idx = jnp.pad(top_target * 16 + top_source, (0, 120)).reshape(1, 128)
    r_blk, r_src, r_top, r_idx = blocks_call(
        blk, blk_src, top_coupling.reshape(64, 128), top_idx
    )
    by_source = (jnp.arange(N)[:, None] == r_src[:, 0, :2].reshape(1, 2 * N)).astype(bf16)
    a = dot(by_source, r_blk.reshape(2 * N, K * K))
    a = a.reshape(N, K, K).transpose(1, 0, 2).reshape(K, N * K)
    a_high, a_low = high_low(a)
    wanted = (me // GROUP) * 16 + jnp.arange(16)
    by_top = (wanted[:, None] == r_idx[:, 0, :8].reshape(1, N)).astype(bf16)
    top_part = dot(by_top, r_top.reshape(N, K * K)).astype(bf16)
    top_part = top_part.reshape(16, K, K).transpose(1, 0, 2).reshape(K, 16 * K)

    basis = leaf_basis.reshape(LEAVES, K, M)
    leaf_t = leaf_transfer.reshape(LEAVES * K, K)
    mid_t = mid_transfer.reshape(GROUP * K, K)
    base_t = base_transfer.reshape(K, K)
    coeffs = upward_call(rows, basis, leaf_t, mid_t, base_t)
    base = field_call(coeffs, top_part, a_high, a_low, base_t)

    near = jnp.pad(near_leaves, ((0, 0), (0, 1)), constant_values=POOL).reshape(-1)
    return near_call(near, source, target, before, rows, after, base, mid_t, leaf_t, basis)


def solution(mesh):
    lead = P(AXIS, None)
    in_specs = (
        P(None, AXIS),
        lead,
        lead,
        lead,
        lead,
        lead,
        lead,
        lead,
        lead,
        P(AXIS),
        lead,
        P(AXIS),
        P(AXIS),
    )
    return jax.shard_map(
        per_device, mesh=mesh, in_specs=in_specs, out_specs=lead, check_vma=False
    )
```

time: 748 us -> 154 us (0.21)
  other arithmetic: 224 us -> 4.44 us
  matrix products: 186 us -> 0.91 us
  local copies, waits for them, and re-layouts: 163 us -> 19.2 us
  Pallas kernels: 0 us -> 109 us
  waiting for transfers between devices: 79.2 us -> 0.01 us
  blocking collectives: 55.9 us -> 0 us
  between operations: 15.5 us -> 0.28 us
    dot_general x35 -> x3, matrix products: 186 us -> 0.91 us  [dot(): return jnp.dot(a, b, preferred_element_type=f32)]
    reduce_sum x28 -> x2, other arithmetic: 168 us -> 1.07 us  [the longest x1 0.94 us: per_device(): rank = jnp.sum((targets[:, None] == targets[None, :]) & earlier, axis=1)]
    gather x56 -> x0, local copies, waits for them, and re-layouts: 121 us -> none  [the longest x27 101 us: near_step(): other_charges = jnp.take(pool_charges, column, axis=0)]
    pallas_call x0 -> x5, Pallas kernels: none -> 109 us  [the longest x1 38 us: near_call(): pl.pallas_call(near_kernel, grid_spec=grid_spec, out_shape=jax.ShapeDtype...]
    all_gather x1 -> x0, waiting for transfers between devices: 65 us -> none  [in_one_piece(): out, at, done = (lax.all_gather(both, axis, axis=dim, tiled=True), 0, [])]
    all_gather x4 -> x0, blocking collectives: 36.7 us -> none  [stacked_from(): pieces = lax.all_gather(pieces, axes[k], axis=0, tiled=True)]
    select_n x57 -> x0, other arithmetic: 22.4 us -> none  [the longest x54 22.4 us: near_step(): other_points = jnp.take(pool_points, column, axis=1)]
    unnamed x55 -> x31, local copies, waits for them, and re-layouts: 27.6 us -> 5.7 us
  transfers between devices with their start and end apart: 9 -> 4, of which waited for: 3 -> 0; matrix products, arithmetic and copies ran while one was open for 74% -> 13% of each run, Pallas kernels for 0% -> 47%
where the time goes in v1:
time: 154 us; the launch traced here: 152 us
  Pallas kernels  109 us (71%)
  local copies, waits for them, and re-layouts  19.2 us (12%)
  starting transfers between devices  17.8 us (12%)
  other arithmetic  4.44 us (3%)
    pallas_call x1, Pallas kernels, near_call(): pl.pallas_call(near_kernel, grid_spec=grid_spec, out_shape=jax.ShapeDtype...  38 us
    pallas_call x1, Pallas kernels, blocks_call(): pl.pallas_call(blocks_kernel, out_shape=(jax.ShapeDtypeStruct(blk.shape,...  37 us
    pallas_call x1, Pallas kernels, field_call(): pl.pallas_call(field_kernel, out_shape=jax.ShapeDtypeStruct((K, RHS), bf1...  19 us
    pallas_call x1, Pallas kernels, feature_call(): pl.pallas_call(functools.partial(feature_kernel, math.sqrt(NNEAR * M)), o...  8.36 us
    ppermute x1, starting transfers between devices, per_device(): after = lax.ppermute(rows, AXIS, down)  7.86 us
    pallas_call x1, Pallas kernels, upward_call(): pl.pallas_call(upward_kernel, grid=(GROUP,), in_specs=[pl.BlockSpec((GROU...  6.67 us
    ppermute x1, starting transfers between devices, per_device(): lax.ppermute(points, AXIS, down)  6.09 us
    unnamed x31, local copies, waits for them, and re-layouts  5.7 us
  transfers between devices with their start and end apart: 4, of which 0 were waited for; matrix products, arithmetic and copies ran while one was open for 13% of the time, Pallas kernels for 47%

profile of v1, /device:TPU:32, one launch (start us, length us, event | category | flops | bytes accessed | tf_op | source)
XLA Modules:
  0.0 151.7 jit_solution(3261275297573364979)
XLA Ops:
  0.0 1.0 copy.33
  1.0 6.1 %collective-permute-start.1 = (f32[3,64,128]{2,1,0:T(8,128)S(1)}, f32[3,64,128]{2,1,0:T(8,128)}, u32[]{:S(2)}, u32[]{:S(2)}) collective-permute-start(f32[3,64,128]{2,1,0:T(8,128)S(1)} %bitcast.34), channel_id=1, source_target_pairs={{1,0},{2,1},{3,2},{4,3},{5,4},{6,5},{7,6},{8,7},{9,8},{10,9},{11,1... | collective-permute-start | bytes 294920 | tf_op jit(solution)/shard_map/ppermute | solution.py:416
  7.1 1.9 %collective-permute-start = (f32[3,64,128]{2,1,0:T(8,128)S(1)}, f32[3,64,128]{2,1,0:T(8,128)}, u32[]{:S(2)}, u32[]{:S(2)}) collective-permute-start(f32[3,64,128]{2,1,0:T(8,128)S(1)} %bitcast.35), channel_id=1, source_target_pairs={{0,1},{1,2},{2,3},{3,4},{4,5},{5,6},{6,7},{7,8},{8,9},{9,10},{10,1... | collective-permute-start | bytes 294920 | tf_op jit(solution)/shard_map/ppermute | solution.py:414
  9.0 7.9 %collective-permute-start.3 = (bf16[64,128,128]{2,1,0:T(8,128)(2,1)}, bf16[64,128,128]{2,1,0:T(8,128)(2,1)}, u32[]{:S(2)}, u32[]{:S(2)}) collective-permute-start(bf16[64,128,128]{2,1,0:T(8,128)(2,1)} %bitcast.27), channel_id=1, source_target_pairs={{1,0},{2,1},{3,2},{4,3},{5,4},{6,5},{7,6},{8,7},{9,8},{10,9},{11,1... | collective-permute-start | bytes 6291464 | tf_op jit(solution)/shard_map/ppermute | solution.py:410
  16.9 1.9 %collective-permute-start.2 = (bf16[64,128,128]{2,1,0:T(8,128)(2,1)}, bf16[64,128,128]{2,1,0:T(8,128)(2,1)}, u32[]{:S(2)}, u32[]{:S(2)}) collective-permute-start(bf16[64,128,128]{2,1,0:T(8,128)(2,1)} %bitcast.28), channel_id=1, source_target_pairs={{0,1},{1,2},{2,3},{3,4},{4,5},{5,6},{6,7},{7,8},{8,9},{9,10},{10,1... | collective-permute-start | bytes 6291464 | tf_op jit(solution)/shard_map/ppermute | solution.py:409
  18.8 0.9 convert_reduce_fusion
  19.8 0.7 fusion.13
  20.5 0.1 multiply_reduce_fusion
  20.6 1.3 reshape.84.top
  21.9 0.1 sub.27
  22.1 0.7 pad.13.blk_src
  22.7 0.4 convolution_convert_fusion
  23.2 1.0 reshape.83.blk
  24.2 0.5 pad_bitcast_fusion.top_idx
  24.7 37.0 %blocks.1 = (bf16[128,16,128]{2,1,0:T(8,128)(2,1)}, s32[128,1,128]{2,1,0:T(1,128)}, bf16[16,64,128]{2,1,0:T(8,128)(2,1)}, s32[16,1,128]{2,1,0:T(1,128)}) custom-call(bf16[128,16,128]{2,1,0:T(8,128)(2,1)} %reshape.83.blk, s32[128,1,128]{2,1,0:T(1,128)} %pad.13.blk_src, bf16[64,128]{1,0:T(8,128)(2,1)} %reshape.84.top, s32[1,128]{1,0:T(1,128)} %pad_bitcast_fusion.top_idx), custom_call_target="tpu_custom_call" | custom-call | flops 100000000 | bytes 1000000 | tf_op jit(solution)/shard_map/blocks/pallas_call | solution.py:191
  61.8 0.7 slice_reduce_fusion.1
  62.5 0.1 eq.66
  62.6 1.0 slice_reduce_fusion
  63.6 0.1 eq.70
  63.7 1.1 reshape.86
  64.8 1.3 reshape.89
  66.1 0.2 copy.25
  66.3 0.3 convolution_bitcast_fusion
  66.6 0.6 copy.26
  67.2 0.0 copy-start.11
  67.2 0.0 copy-start.9
  67.2 0.0 copy-start.8
  67.2 1.0 reshape.90
  68.2 0.8 subtract_convert_fusion
  69.1 0.2 convolution_convert_fusion.1
  69.3 0.7 reshape.82.base_t
  70.0 0.1 copy.27
  70.1 0.1 reshape.76.near
  70.2 0.7 reshape.81.mid_t
  71.0 0.1 reshape.87
  71.1 0.1 copy.32
  71.2 0.8 reshape.88.top_part
  71.9 1.2 reshape.80.leaf_t
  73.1 0.9 copy.29
  74.0 0.1 pad.18.clone
  74.1 6.7 %upward.1.coeffs = bf16[2,32,128]{2,1,0:T(8,128)(2,1)} custom-call(bf16[64,128,128]{2,1,0:T(8,128)(2,1)} %bitcast.29, bf16[64,32,128]{2,1,0:T(8,128)(2,1)} %bitcast.24, bf16[2048,32]{1,0:T(8,128)(2,1)} %reshape.80.leaf_t, bf16[256,32]{1,0:T(8,128)(2,1)} %reshape.81.mid_t, bf16[32,32]{1,0:T(8,128)(2,1)} %reshape.82.base_t), custom_call_target="tpu_custom_call" | custom-call | flops 100000000 | bytes 3000000 | tf_op jit(solution)/shard_map/upward/pallas_call | solution.py:116
  80.7 19.0 %field.1.base = bf16[32,128]{1,0:T(8,128)(2,1)} custom-call(bf16[2,32,128]{2,1,0:T(8,128)(2,1)} %upward.1.coeffs, bf16[32,512]{1,0:T(8,128)(2,1)} %reshape.88.top_part, bf16[32,4096]{1,0:T(8,128)(2,1)} %get-tuple-element.18.a_high, bf16[32,4096]{1,0:T(8,128)(2,1)} %get-tuple-element.17.a_low, bf16[32,32]{1,0:T(8,128)(2,1)} %reshape.82.base_t), custom_call_target="tpu_custom_call" | custom-call | flops 100000000 | bytes 1000000 | tf_op jit(solution)/shard_map/field/pallas_call | solution.py:291
  99.8 1.8 %maximum_maximum_fusion.points = f32[3,200,128]{2,1,0:T(8,128)} fusion(f32[3,64,128]{2,1,0:T(8,128)} %collective-permute-done.1, f32[3,64,128]{2,1,0:T(8,128)S(1)} %bitcast.36, f32[3,64,128]{2,1,0:T(8,128)} %collective-permute-done, f32[200]{0:T(256)S(1)} %pad.18.clone), kind=kLoop, calls=%fused_computation.4 | loop fusion | flops 230400 | bytes 602912 | tf_op jit(solution)/shard_map/concatenate | solution.py:412
  101.6 8.4 %features.1 = (bf16[200,32,128]{2,1,0:T(8,128)(2,1)}, bf16[64,128,32]{2,1,0:T(8,128)(2,1)}) custom-call(f32[3,200,128]{2,1,0:T(8,128)} %maximum_maximum_fusion.points), custom_call_target="tpu_custom_call" | custom-call | flops 100000000 | bytes 1000000 | tf_op jit(solution)/shard_map/features/pallas_call | solution.py:88
  110.0 0.7 copy-done.4
  110.7 1.6 %copy-done.5 = bf16[64,128,32]{2,1,0:T(8,128)(2,1)S(1)} copy-done((bf16[64,128,32]{2,1,0:T(8,128)(2,1)S(1)}, bf16[64,128,32]{2,1,0:T(8,128)(2,1)}, u32[]{:S(2)}) %copy-start.5) | copy-done | bytes 524312
  112.3 1.4 copy-done.6
  113.7 38.0 %near.1 = bf16[8192,128]{1,0:T(8,128)(2,1)} custom-call(s32[1792]{0:T(1024)S(1)} %reshape.76.near, bf16[200,32,128]{2,1,0:T(8,128)(2,1)S(1)} %copy-done.6, bf16[64,128,32]{2,1,0:T(8,128)(2,1)S(1)} %copy-done.5, bf16[64,128,128]{2,1,0:T(8,128)(2,1)} %collective-permute-done.2.before, bf16[64,128,128]{2,1,0:T(8,128)(2,1)} %bitcast.30, ...), custom_call_target="tpu_custom_call" | custom-call | flops 10000000000 | bytes 10000000 | tf_op jit(solution)/shard_map/near/pallas_call | solution.py:371
  (32 shorter events, 0.1 us)
Async XLA Ops:
  0.0 22.7 %copy-start = (bf16[189,1024]{1,0:T(8,128)(2,1)S(1)}, bf16[189,1024]{1,0:T(8,128)(2,1)}, u32[]{:S(2)}) copy-start(bf16[189,1024]{1,0:T(8,128)(2,1)} %param.20) | copy-start | bytes 1161220
  0.0 24.2 %copy-start.12 = (s32[8]{0:T(128)S(1)}, s32[8]{0:T(128)}, u32[]{:S(2)}) copy-start(s32[8]{0:T(128)} %param.25) | copy-start | bytes 100
  0.0 24.2 %copy-start.13 = (s32[8]{0:T(128)S(1)}, s32[8]{0:T(128)}, u32[]{:S(2)}) copy-start(s32[8]{0:T(128)} %param.24) | copy-start | bytes 100
  1.0 98.8 %collective-permute-start.1 = (f32[3,64,128]{2,1,0:T(8,128)S(1)}, f32[3,64,128]{2,1,0:T(8,128)}, u32[]{:S(2)}, u32[]{:S(2)}) collective-permute-start(f32[3,64,128]{2,1,0:T(8,128)S(1)} %bitcast.34), channel_id=1, source_target_pairs={{1,0},{2,1},{3,2},{4,3},{5,4},{6,5},{7,6},{8,7},{9,8},{10,9},{11,1... | collective-permute-start | bytes 294920 | tf_op jit(solution)/shard_map/ppermute | solution.py:416
  7.1 92.7 %collective-permute-start = (f32[3,64,128]{2,1,0:T(8,128)S(1)}, f32[3,64,128]{2,1,0:T(8,128)}, u32[]{:S(2)}, u32[]{:S(2)}) collective-permute-start(f32[3,64,128]{2,1,0:T(8,128)S(1)} %bitcast.35), channel_id=1, source_target_pairs={{0,1},{1,2},{2,3},{3,4},{4,5},{5,6},{6,7},{7,8},{8,9},{9,10},{10,1... | collective-permute-start | bytes 294920 | tf_op jit(solution)/shard_map/ppermute | solution.py:414
  9.0 101.0 %collective-permute-start.3 = (bf16[64,128,128]{2,1,0:T(8,128)(2,1)}, bf16[64,128,128]{2,1,0:T(8,128)(2,1)}, u32[]{:S(2)}, u32[]{:S(2)}) collective-permute-start(bf16[64,128,128]{2,1,0:T(8,128)(2,1)} %bitcast.27), channel_id=1, source_target_pairs={{1,0},{2,1},{3,2},{4,3},{5,4},{6,5},{7,6},{8,7},{9,8},{10,9},{11,1... | collective-permute-start | bytes 6291464 | tf_op jit(solution)/shard_map/ppermute | solution.py:410
  16.9 93.1 %collective-permute-start.2 = (bf16[64,128,128]{2,1,0:T(8,128)(2,1)}, bf16[64,128,128]{2,1,0:T(8,128)(2,1)}, u32[]{:S(2)}, u32[]{:S(2)}) collective-permute-start(bf16[64,128,128]{2,1,0:T(8,128)(2,1)} %bitcast.28), channel_id=1, source_target_pairs={{0,1},{1,2},{2,3},{3,4},{4,5},{5,6},{6,7},{7,8},{8,9},{9,10},{10,1... | collective-permute-start | bytes 6291464 | tf_op jit(solution)/shard_map/ppermute | solution.py:409
  67.2 2.1 %copy-start.11 = (bf16[1,1024]{1,0:T(2,128)(2,1)S(1)}, bf16[1,1024]{1,0:T(2,128)(2,1)}, u32[]{:S(2)}) copy-start(bf16[1,1024]{1,0:T(2,128)(2,1)} %param.19) | copy-start | bytes 6148
  67.2 2.8 %copy-start.9 = (s32[64,27]{0,1:T(8,128)S(1)}, s32[64,27]{0,1:T(8,128)}, u32[]{:S(2)}) copy-start(s32[64,27]{0,1:T(8,128)} %param.15) | copy-start | bytes 20740
  67.2 3.0 %copy-start.10 = (bf16[8,1024]{1,0:T(8,128)(2,1)S(1)}, bf16[8,1024]{1,0:T(8,128)(2,1)}, u32[]{:S(2)}) copy-start(bf16[8,1024]{1,0:T(8,128)(2,1)} %param.18) | copy-start | bytes 49156
  67.2 4.7 %copy-start.8 = (bf16[64,1024]{1,0:T(8,128)(2,1)S(1)}, bf16[64,1024]{1,0:T(8,128)(2,1)}, u32[]{:S(2)}) copy-start(bf16[64,1024]{1,0:T(8,128)(2,1)} %param.17) | copy-start | bytes 393220
  68.2 4.9 %copy-start.7 = (bf16[64,4096]{1,0:T(8,128)(2,1)S(1)}, bf16[64,4096]{1,0:T(8,128)(2,1)}, u32[]{:S(2)}) copy-start(bf16[64,4096]{1,0:T(8,128)(2,1)} %param.16) | copy-start | bytes 1572868
  74.1 35.9 %copy-start.1 = (bf16[2048,32]{1,0:T(8,128)(2,1)S(1)}, bf16[2048,32]{1,0:T(8,128)(2,1)}, u32[]{:S(2)}) copy-start(bf16[2048,32]{1,0:T(8,128)(2,1)} %reshape.80.leaf_t) | copy-start | bytes 393220
  74.1 35.9 %copy-start.2 = (bf16[8,8,32,128]{3,2,1,0:T(8,128)(2,1)S(1)}, bf16[8,8,32,128]{3,2,1,0:T(8,128)(2,1)}, u32[]{:S(2)}) copy-start(bf16[8,8,32,128]{3,2,1,0:T(8,128)(2,1)} %copy.29) | copy-start | bytes 1572868
  74.1 35.9 %copy-start.3 = (bf16[256,32]{1,0:T(8,128)(2,1)S(1)}, bf16[256,32]{1,0:T(8,128)(2,1)}, u32[]{:S(2)}) copy-start(bf16[256,32]{1,0:T(8,128)(2,1)} %reshape.81.mid_t) | copy-start | bytes 49156
  110.0 0.7 copy-start.4
  110.7 1.6 %copy-start.5 = (bf16[64,128,32]{2,1,0:T(8,128)(2,1)S(1)}, bf16[64,128,32]{2,1,0:T(8,128)(2,1)}, u32[]{:S(2)}) copy-start(bf16[64,128,32]{2,1,0:T(8,128)(2,1)} %get-tuple-element.12.target) | copy-start | bytes 1572868
  112.3 1.4 copy-start.6

commit v2 on v1

v2 whole, which is shorter than its diff:
```python
import functools
import math

import jax
import jax.numpy as jnp
from jax import lax
from jax.experimental import pallas as pl
from jax.experimental.pallas import tpu as pltpu
from jax.sharding import PartitionSpec as P

K = 32
RHS = 128
M = 128
N = 128
LEAVES = 64
POOL = 3 * LEAVES
NNEAR = 27
PAIRS = (NNEAR + 1) // 2
GROUP = 8
DELTA_SQ = 0.0025
AXIS = "leaf"
MESH = pl.DeviceIdType.MESH
bf16 = jnp.bfloat16
f32 = jnp.float32


def dot(a, b):
    return jnp.dot(a, b, preferred_element_type=f32)


def dot_t(a, b):
    return lax.dot_general(a, b, (((0,), (0,)), ((), ())), preferred_element_type=f32)


def vmem(*shape):
    return pl.BlockSpec(shape, lambda *_: (0,) * len(shape))


def split3(v):
    high = v.astype(bf16).astype(f32)
    rest = v - high
    mid = rest.astype(bf16).astype(f32)
    return high, mid, rest - mid


def features(scale, points, target):
    centred = [(p - 0.5) * scale for p in points]
    norm = centred[0] * centred[0] + centred[1] * centred[1] + centred[2] * centred[2]
    one = jnp.ones_like(norm)
    rows = []
    for c in centred:
        h, m, l = split3(c)
        if target:
            h, m, l = -2.0 * h, -2.0 * m, -2.0 * l
            rows += [h, h, m, m, h, l]
        else:
            rows += [h, m, h, m, l, h]
    if target:
        rows += [*split3(norm + scale * scale * DELTA_SQ), one, one, one]
    else:
        rows += [one, one, one, *split3(norm)]
    return rows + [jnp.zeros_like(norm)] * (K - len(rows))


def exchange_kernel(
    scale,
    blk,
    blk_src,
    top,
    top_idx,
    points,
    charges,
    basis,
    leaf_t,
    mid_t,
    base_t,
    r_blk,
    r_src,
    every,
    top_all,
    tops,
    source,
    target,
    held,
    r_top,
    r_idx,
    lifted,
    coeffs,
    mine,
    mids,
    part,
    others,
    lines,
    send,
    recv,
    local,
):
    me = lax.axis_index(AXIS)
    plane, place = me // GROUP, me % GROUP
    core, y = place % 2, place // 2
    fetch = pltpu.make_async_copy(charges, held, local.at[0])
    fetch.start()
    barrier = pltpu.get_barrier_semaphore()

    def hello(o, c):
        pl.semaphore_signal(
            barrier, inc=1, device_id=(lax.rem(me + o, N),), device_id_type=MESH
        )
        return c

    lax.fori_loop(1, N, hello, 0)
    pl.semaphore_wait(barrier, N - 1)

    def remote(src, dst, k, to):
        return pltpu.make_async_remote_copy(
            src_ref=src,
            dst_ref=dst,
            send_sem=send.at[k],
            recv_sem=recv.at[k],
            device_id=(to,),
            device_id_type=MESH,
        )

    def finish(ref, k):
        whole = remote(ref, ref, k, me)
        whole.wait_send()
        whole.wait_recv()

    right, left = lax.rem(me + 1, N), lax.rem(me + N - 1, N)
    to_right = remote(points, others.at[0], 0, right)
    to_left = remote(points, others.at[1], 1, left)
    to_right.start()
    to_left.start()

    def give_top(o, c):
        to = lax.rem(plane + o, 16) * GROUP + place
        remote(top, r_top.at[plane], 2, to).start()
        remote(top_idx, r_idx.at[plane], 3, to).start()
        return c

    lax.fori_loop(1, 16, give_top, 0)

    def give(o, c):
        to = lax.rem(me + o, N)
        remote(blk.at[to], r_blk.at[me], 4, to).start()
        remote(blk_src.at[to], r_src.at[me], 5, to).start()
        return c

    lax.fori_loop(1, N, give, 0)
    own = [
        pltpu.make_async_copy(blk.at[me], r_blk.at[me], local.at[1]),
        pltpu.make_async_copy(blk_src.at[me], r_src.at[me], local.at[2]),
        pltpu.make_async_copy(top, r_top.at[plane], local.at[3]),
        pltpu.make_async_copy(top_idx, r_idx.at[plane], local.at[4]),
    ]
    for copy in own:
        copy.start()

    fetch.wait()

    def one_mid(m, c):
        rows = []
        for b in range(GROUP):
            rows.append(dot(basis[m * GROUP + b], held[m * GROUP + b]).astype(bf16))
        first = pl.multiple_of(m * GROUP * K, GROUP * K)
        rows = dot_t(leaf_t[pl.ds(first, GROUP * K), :], jnp.concatenate(rows, axis=0))
        mids[pl.ds(pl.multiple_of(m * K, K), K), :] = rows.astype(bf16)
        return c

    lax.fori_loop(0, GROUP, one_mid, 0)
    base = dot_t(mid_t[...], mids[...]).astype(bf16)
    coeffs[0] = base
    coeffs[1] = dot_t(base_t[...], base).astype(bf16)
    for o in range(1, 4):
        to = plane * GROUP + lax.rem(y + o, 4) * 2 + core
        remote(coeffs.at[0], every.at[core, plane, y], 6, to).start()
    for o in range(1, GROUP):
        to = plane * GROUP + lax.rem(place + o, GROUP)
        remote(coeffs.at[1], lifted.at[place], 7, to).start()
    own += [
        pltpu.make_async_copy(coeffs.at[0], every.at[core, plane, y], local.at[5]),
        pltpu.make_async_copy(coeffs.at[1], lifted.at[place], local.at[6]),
    ]
    for copy in own[4:]:
        copy.start()

    def side(rows, put, count):
        for r, row in enumerate(rows):
            lines[pl.ds(r, LEAVES, stride=K), :] = row
        lax.fori_loop(0, count, put, 0, unroll=4)

    def line(l):
        return lines[pl.ds(pl.multiple_of(l * K, K), K), :]

    def put_target(l, c):
        target[l] = line(l).T.astype(bf16)
        return c

    def put_source(block):
        def put(l, c):
            source[block * LEAVES + l] = line(l).astype(bf16)
            return c

        return put

    here = [points[i] for i in range(3)]
    side(features(scale, here, True), put_target, LEAVES)
    for copy in own:
        copy.wait()
    finish(lifted.at[pl.ds(0, 3)], 6)
    for o in range(1, 16):
        to = lax.rem(plane + o, 16) * GROUP + place
        remote(every.at[core, plane], every.at[core, plane], 8, to).start()
    finish(lifted.at[pl.ds(0, GROUP - 1)], 7)
    mine[...] = jnp.sum(lifted[...].astype(f32), axis=0).astype(bf16)
    for o in range(1, 16):
        to = lax.rem(plane + o, 16) * GROUP + place
        remote(mine, top_all.at[plane], 9, to).start()
    own_top = pltpu.make_async_copy(mine, top_all.at[plane], local.at[0])
    own_top.start()
    side(features(scale, here, False), put_source(1), LEAVES)
    own_top.wait()

    finish(r_top.at[pl.ds(0, 15)], 2)
    finish(r_idx.at[pl.ds(0, 15)], 3)
    named = jnp.sum(r_idx[...], axis=0)
    wanted = plane * 16 + lax.broadcasted_iota(jnp.int32, (16, N), 0)
    chosen = jnp.where(wanted == named, 1.0, 0.0).astype(bf16)
    part[...] = dot(chosen, r_top[...].reshape(N, K * K)).astype(bf16)
    for o in range(1, GROUP):
        to = plane * GROUP + lax.rem(place + o, GROUP)
        remote(part, tops.at[place], 10, to).start()
    own_part = pltpu.make_async_copy(part, tops.at[place], local.at[0])
    own_part.start()
    to_right.wait()
    to_left.wait()
    spare = source[LEAVES]
    for l in range(8):
        source[POOL + l] = spare
    side(features(scale, [others[0, i] for i in range(3)], False), put_source(0), LEAVES)
    finish(every.at[0, pl.ds(0, 15)], 8)
    across = remote(every.at[core], every.at[core], 11, me + 1 - 2 * core)
    across.start()
    side(features(scale, [others[1, i] for i in range(3)], False), put_source(2), LEAVES)
    finish(top_all.at[pl.ds(0, 15)], 9)
    own_part.wait()
    finish(tops.at[pl.ds(0, GROUP - 1)], 10)
    across.wait()
    finish(r_blk.at[pl.ds(0, N - 1)], 4)
    finish(r_src.at[pl.ds(0, N - 1)], 5)


def exchange_call(blk, blk_src, top, top_idx, points, charges, basis, leaf_t, mid_t, base_t):
    inside = pl.BlockSpec(memory_space=pltpu.VMEM)
    shape = jax.ShapeDtypeStruct
    return pl.pallas_call(
        functools.partial(exchange_kernel, math.sqrt(NNEAR * M)),
        out_shape=(
            shape(blk.shape, bf16),
            shape(blk_src.shape, jnp.int32),
            shape((2, 16, 4, K, RHS), bf16),
            shape((16, K, RHS), bf16),
            shape((GROUP, 16, K * K), bf16),
            shape((POOL + 8, K, M), bf16),
            shape((LEAVES, M, K), bf16),
        ),
        in_specs=[inside] * 5 + [pl.BlockSpec(memory_space=pl.ANY)] + [inside] * 4,
        out_specs=(inside,) * 7,
        scratch_shapes=[
            pltpu.VMEM((LEAVES, M, RHS), bf16),
            pltpu.VMEM((16, 8, K * K), bf16),
            pltpu.VMEM((16, 1, N), jnp.int32),
            pltpu.VMEM((GROUP, K, RHS), bf16),
            pltpu.VMEM((2, K, RHS), bf16),
            pltpu.VMEM((K, RHS), bf16),
            pltpu.VMEM((GROUP * K, RHS), bf16),
            pltpu.VMEM((16, K * K), bf16),
            pltpu.VMEM((2, 3, LEAVES, M), f32),
            pltpu.VMEM((LEAVES * K, M), f32),
            pltpu.SemaphoreType.DMA((12,)),
            pltpu.SemaphoreType.DMA((12,)),
            pltpu.SemaphoreType.DMA((7,)),
        ],
        compiler_params=pltpu.CompilerParams(
            collective_id=0, has_side_effects=True, vmem_limit_bytes=40 * 1024 * 1024
        ),
        cost_estimate=pl.CostEstimate(flops=10**9, bytes_accessed=10**7, transcendentals=0),
        name="exchange",
    )(blk, blk_src, top, top_idx, points, charges, basis, leaf_t, mid_t, base_t)


def near_kernel(
    near,
    source,
    target,
    before,
    here,
    after,
    a_high,
    a_low,
    every,
    t_high,
    t_low,
    top_all,
    base_t,
    mid_t,
    leaf_t,
    basis,
    out,
    pool,
    kern,
    gathered,
    base,
    sems,
):
    step = pl.program_id(0)

    @pl.when(step == 0)
    def _():
        copies = [
            pltpu.make_async_copy(ref, pool.at[pl.ds(LEAVES * i, LEAVES)], sems.at[i])
            for i, ref in enumerate((before, here, after))
        ]
        for copy in copies:
            copy.start()
        pool[POOL] = jnp.zeros((M, RHS), bf16)
        top_field = (dot(t_high[...], top_all[...]) + dot(t_low[...], top_all[...])).astype(bf16)
        coupled = dot(a_high[...], every[...]) + dot(a_low[...], every[...])
        base[...] = (coupled + dot(base_t[...], top_field)).astype(bf16)
        for copy in copies:
            copy.wait()

    mid = dot(mid_t[...], base[...]).astype(bf16)
    fields = dot(leaf_t[...], mid).astype(bf16)
    for b in range(GROUP):
        leaf = step * GROUP + b
        mine = target[b]
        for j in range(PAIRS):
            one = near[leaf * 2 * PAIRS + 2 * j]
            two = near[leaf * 2 * PAIRS + 2 * j + 1]
            others = jnp.concatenate([source[one], source[two]], axis=1)
            squares = dot(mine, others)
            kern[b, :, 2 * M * j : 2 * M * (j + 1)] = lax.rsqrt(squares.astype(bf16))
            gathered[b, 2 * M * j : 2 * M * j + M] = pool[one]
            gathered[b, 2 * M * j + M : 2 * M * (j + 1)] = pool[two]
        far = dot_t(basis[b], fields[b * K : (b + 1) * K])
        total = dot(kern[b], gathered[b]) + far
        out[pl.ds(b * M, M), :] = total.astype(bf16)


def near_call(near, source, target, before, here, after, far, mid_t, leaf_t, basis):
    count = source.shape[0]
    grid_spec = pltpu.PrefetchScalarGridSpec(
        num_scalar_prefetch=1,
        grid=(LEAVES // GROUP,),
        in_specs=[
            vmem(count, K, M),
            pl.BlockSpec((GROUP, M, K), lambda i, _: (i, 0, 0)),
            pl.BlockSpec(memory_space=pl.ANY),
            pl.BlockSpec(memory_space=pl.ANY),
            pl.BlockSpec(memory_space=pl.ANY),
            *[vmem(*v.shape) for v in far],
            pl.BlockSpec((K, K), lambda i, _: (i, 0)),
            pl.BlockSpec((GROUP * K, K), lambda i, _: (i, 0)),
            pl.BlockSpec((GROUP, K, M), lambda i, _: (i, 0, 0)),
        ],
        out_specs=pl.BlockSpec((GROUP * M, RHS), lambda i, _: (i, 0)),
        scratch_shapes=[
            pltpu.VMEM((POOL + 1, M, RHS), bf16),
            pltpu.VMEM((GROUP, M, 2 * M * PAIRS), bf16),
            pltpu.VMEM((GROUP, 2 * M * PAIRS, RHS), bf16),
            pltpu.VMEM((K, RHS), bf16),
            pltpu.SemaphoreType.DMA((3,)),
        ],
    )
    return pl.pallas_call(
        near_kernel,
        grid_spec=grid_spec,
        out_shape=jax.ShapeDtypeStruct((LEAVES * M, RHS), bf16),
        compiler_params=pltpu.CompilerParams(
            vmem_limit_bytes=48 * 1024 * 1024, dimension_semantics=("arbitrary",)
        ),
        cost_estimate=pl.CostEstimate(
            flops=10**10, bytes_accessed=10**7, transcendentals=3 * 10**7
        ),
        name="near",
    )(near, source, target, before, here, after, *far, mid_t, leaf_t, basis)


def high_low(v):
    high = v.astype(bf16)
    return high, (v - high.astype(f32)).astype(bf16)


def per_device(
    coords,
    charges,
    near_leaves,
    leaf_basis,
    leaf_transfer,
    mid_transfer,
    base_transfer,
    base_coupling,
    base_target,
    base_source,
    top_coupling,
    top_target,
    top_source,
):
    me = lax.axis_index(AXIS)
    up = [(i, i + 1) for i in range(N - 1)]
    down = [(i + 1, i) for i in range(N - 1)]
    rows = charges.reshape(LEAVES, M, RHS)
    before = lax.ppermute(rows, AXIS, up)
    after = lax.ppermute(rows, AXIS, down)
    points = coords.reshape(3, LEAVES, M)

    targets = base_target[:, 0]
    count = targets.shape[0]
    earlier = jnp.arange(count)[:, None] > jnp.arange(count)[None, :]
    rank = jnp.sum((targets[:, None] == targets[None, :]) & earlier, axis=1)
    slots = jnp.arange(2 * N)
    chosen = (slots[:, None] == (2 * targets + rank)[None, :]).astype(bf16)
    blk = dot(chosen, base_coupling).astype(bf16).reshape(N, 16, 128)
    order = (base_source % 2) * 64 + (base_source // 8) * 4 + (base_source // 2) % 4
    slot_source = jnp.sum(chosen.astype(jnp.int32) * (order + 1)[None, :], axis=1) - 1
    blk_src = jnp.pad(slot_source.reshape(N, 1, 2), ((0, 0), (0, 0), (0, 126)))
    lane = jnp.arange(N)
    top_idx = jnp.tile(top_target * 16 + top_source, 16)
    top_idx = jnp.where(lane // 8 == me // GROUP, top_idx, 0).reshape(1, N)

    basis = leaf_basis.reshape(LEAVES, K, M)
    leaf_t = leaf_transfer.reshape(LEAVES * K, K)
    mid_t = mid_transfer.reshape(GROUP * K, K)
    base_t = base_transfer.reshape(K, K)
    r_blk, r_src, every, top_all, tops, source, target = exchange_call(
        blk, blk_src, top_coupling, top_idx, points, rows, basis, leaf_t, mid_t, base_t
    )
    by_source = (lane[:, None] == r_src[:, 0, :2].reshape(1, 2 * N)).astype(bf16)
    a = dot(by_source, r_blk.reshape(2 * N, K * K))
    a = a.reshape(N, K, K).transpose(1, 0, 2).reshape(K, N * K)
    t = jnp.sum(tops.astype(f32), axis=0)
    t = t.reshape(16, K, K).transpose(1, 0, 2).reshape(K, 16 * K)
    far = (
        *high_low(a),
        every.reshape(N * K, RHS),
        *high_low(t),
        top_all.reshape(16 * K, RHS),
        base_t,
    )
    near = jnp.pad(near_leaves, ((0, 0), (0, 1)), constant_values=POOL).reshape(-1)
    return near_call(near, source, target, before, rows, after, far, mid_t, leaf_t, basis)


def solution(mesh):
    lead = P(AXIS, None)
    in_specs = (
        P(None, AXIS),
        lead,
        lead,
        lead,
        lead,
        lead,
        lead,
        lead,
        lead,
        P(AXIS),
        lead,
        P(AXIS),
        P(AXIS),
    )
    return jax.shard_map(
        per_device, mesh=mesh, in_specs=in_specs, out_specs=lead, check_vma=False
    )
```

time: 154 us -> 113 us (0.73)
  the two profiles are of different devices: /device:TPU:32 before, /device:TPU:1 now
where the time goes in v2:
time: 113 us
  Pallas kernels  86 us (76%)
  local copies, waits for them, and re-layouts  16 us (14%)
  starting transfers between devices  6.64 us (6%)
  other arithmetic  3.28 us (3%)
    pallas_call x1, Pallas kernels, exchange_call(): pl.pallas_call(functools.partial(exchange_kernel, math.sqrt(NNEAR * M)),...  46.5 us
    pallas_call x1, Pallas kernels, near_call(): pl.pallas_call(near_kernel, grid_spec=grid_spec, out_shape=jax.ShapeDtype...  39.5 us
    unnamed x23, local copies, waits for them, and re-layouts  8.42 us
    ppermute x1, starting transfers between devices, per_device(): after = lax.ppermute(rows, AXIS, down)  3.41 us
    ppermute x1, starting transfers between devices, per_device(): before = lax.ppermute(rows, AXIS, up)  3.23 us
    reshape x1, local copies, waits for them, and re-layouts, per_device(): a = a.reshape(N, K, K).transpose(1, 0, 2).reshape(K, N * K)  2.63 us
  transfers between devices with their start and end apart: 2, of which 0 were waited for; matrix products, arithmetic and copies ran while one was open for 12% of the time, Pallas kernels for 41%

profile of v2, /device:TPU:1, one launch (start us, length us, event | category | flops | bytes accessed | tf_op | source)
XLA Modules:
  0.0 112.9 jit_solution(13625571983998439438)
XLA Ops:
  0.0 0.0 copy-start
  0.0 0.0 copy-start.9
  0.0 3.4 %collective-permute-start.1 = (bf16[64,128,128]{2,1,0:T(8,128)(2,1)}, bf16[64,128,128]{2,1,0:T(8,128)(2,1)}, u32[]{:S(2)}, u32[]{:S(2)}) collective-permute-start(bf16[64,128,128]{2,1,0:T(8,128)(2,1)} %bitcast.23), channel_id=1, source_target_pairs={{1,0},{2,1},{3,2},{4,3},{5,4},{6,5},{7,6},{8,7},{9,8},{10,9},{11,1... | collective-permute-start | bytes 6291464 | tf_op jit(solution)/shard_map/ppermute | solution.py:415
  3.4 3.2 %collective-permute-start = (bf16[64,128,128]{2,1,0:T(8,128)(2,1)}, bf16[64,128,128]{2,1,0:T(8,128)(2,1)}, u32[]{:S(2)}, u32[]{:S(2)}) collective-permute-start(bf16[64,128,128]{2,1,0:T(8,128)(2,1)} %bitcast.24), channel_id=1, source_target_pairs={{0,1},{1,2},{2,3},{3,4},{4,5},{5,6},{6,7},{7,8},{8,9},{9,10},{10,1... | collective-permute-start | bytes 6291464 | tf_op jit(solution)/shard_map/ppermute | solution.py:414
  6.7 0.9 convert_reduce_fusion.1
  7.6 0.7 fusion.10
  8.3 0.1 multiply_reduce_fusion
  8.5 0.7 reduce
  9.2 0.1 reshape.124.base_t
  9.3 0.7 multiply_add_fusion.1
  10.0 0.1 tile.10
  10.0 0.8 copy.26
  10.9 0.1 reshape.117.near
  11.0 0.0 copy-start.2
  11.0 0.1 sub.35
  11.2 0.8 reshape.123.mid_t
  12.0 0.9 copy.30
  12.9 0.0 copy-done
  12.9 0.4 convolution_convert_fusion
  13.4 0.2 reshape.118.blk
  13.6 0.0 copy-done.9
  13.6 0.4 reshape.122.leaf_t
  14.0 0.0 copy-done.8
  14.0 0.1 copy.28
  14.1 0.0 copy-done.2
  14.1 0.0 copy-start.1
  14.1 1.6 %copy-done.1 = bf16[8192,128]{1,0:T(8,128)(2,1)S(1)} copy-done((bf16[8192,128]{1,0:T(8,128)(2,1)S(1)}, bf16[8192,128]{1,0:T(8,128)(2,1)}, u32[]{:S(2)}) %copy-start.1) | copy-done | bytes 2097176
  15.7 46.5 %exchange.1 = (bf16[128,16,128]{2,1,0:T(8,128)(2,1)S(1)}, s32[128,1,128]{2,1,0:T(1,128)S(1)}, bf16[2,16,4,32,128]{4,3,2,1,0:T(8,128)(2,1)S(1)}, bf16[16,32,128]{...) custom-call(bf16[128,16,128]{2,1,0:T(8,128)(2,1)S(1)} %reshape.118.b, ...), custom_call_target="tpu_custom_call" | custom-call | flops 1000000000 | bytes 10000000 | tf_op jit(solution)/shard_map/exchange/pallas_call | solution.py:256
  62.2 0.0 copy-start.3
  62.2 1.3 %copy-done.3 = bf16[64,128,32]{2,1,0:T(8,128)(2,1)} copy-done((bf16[64,128,32]{2,1,0:T(8,128)(2,1)}, bf16[64,128,32]{2,1,0:T(8,128)(2,1)S(1)}, u32[]{:S(2)}) %copy-start.3) | copy-done | bytes 524312
  63.5 1.2 %copy-done.4 = bf16[200,32,128]{2,1,0:T(8,128)(2,1)} copy-done((bf16[200,32,128]{2,1,0:T(8,128)(2,1)}, bf16[200,32,128]{2,1,0:T(8,128)(2,1)S(1)}, u32[]{:S(2)}) %copy-start.4) | copy-done | bytes 1638424
  64.7 1.1 copy-done.6
  65.8 0.2 slice_reduce_fusion
  66.0 0.1 eq.66
  66.1 0.1 reshape.128
  66.3 0.2 copy.25
  66.4 0.1 reshape.129
  66.6 0.2 reshape.125
  66.8 0.2 copy.23
  67.0 0.3 convolution_bitcast_fusion
  67.3 1.9 %copy.24 = f32[32,128,32]{2,1,0:T(8,128)} copy(f32[32,128,32]{1,2,0:T(8,128)S(1)} %convolution_bitcast_fusion) | data formatting | bytes 1048576 | tf_op jit(solution)/shard_map/transpose | solution.py:441
  69.2 2.6 %reshape.126 = f32[32,4096]{1,0:T(8,128)S(1)} reshape(f32[32,128,32]{2,1,0:T(8,128)} %copy.24) | data formatting | bytes 1048576 | tf_op jit(solution)/shard_map/reshape | solution.py:441
  71.9 0.0 collective-permute-done.1.after
  71.9 0.0 collective-permute-done.before
  72.0 0.0 copy-done.7
  72.0 0.0 copy-start.5
  72.0 1.4 %copy-done.5 = bf16[200,32,128]{2,1,0:T(8,128)(2,1)S(1)} copy-done((bf16[200,32,128]{2,1,0:T(8,128)(2,1)S(1)}, bf16[200,32,128]{2,1,0:T(8,128)(2,1)}, u32[]{:S(2)}) %copy-start.5) | copy-done | bytes 1638424
  73.4 39.5 %near.1 = bf16[8192,128]{1,0:T(8,128)(2,1)} custom-call(s32[1792]{0:T(1024)S(1)} %reshape.117.near, bf16[200,32,128]{2,1,0:T(8,128)(2,1)S(1)} %copy-done.5, bf16[64,128,32]{2,1,0:T(8,128)(2,1)} %copy-done.3, bf16[64,128,128]{2,1,0:T(8,128)(2,1)} %collective-permute-done.before, bf16[64,128,128]{2,1,0:T(8,128)(2,1)} %bitcast.25, ...), custom_call_target="tpu_custom_call" | custom-call | flops 10000000000 | bytes 10000000 | tf_op jit(solution)/shard_map/near/pallas_call | solution.py:376
  (12 shorter events, 0.2 us)
Async XLA Ops:
  0.0 12.9 %copy-start = (bf16[189,1024]{1,0:T(8,128)(2,1)S(1)}, bf16[189,1024]{1,0:T(8,128)(2,1)}, u32[]{:S(2)}) copy-start(bf16[189,1024]{1,0:T(8,128)(2,1)} %param.20) | copy-start | bytes 1161220
  0.0 13.6 %copy-start.9 = (bf16[64,1024]{1,0:T(8,128)(2,1)S(1)}, bf16[64,1024]{1,0:T(8,128)(2,1)}, u32[]{:S(2)}) copy-start(bf16[64,1024]{1,0:T(8,128)(2,1)} %param.17) | copy-start | bytes 393220
  0.0 14.0 %copy-start.8 = (bf16[64,4096]{1,0:T(8,128)(2,1)S(1)}, bf16[64,4096]{1,0:T(8,128)(2,1)}, u32[]{:S(2)}) copy-start(bf16[64,4096]{1,0:T(8,128)(2,1)} %param.16) | copy-start | bytes 1572868
  0.0 71.9 %collective-permute-start.1 = (bf16[64,128,128]{2,1,0:T(8,128)(2,1)}, bf16[64,128,128]{2,1,0:T(8,128)(2,1)}, u32[]{:S(2)}, u32[]{:S(2)}) collective-permute-start(bf16[64,128,128]{2,1,0:T(8,128)(2,1)} %bitcast.23), channel_id=1, source_target_pairs={{1,0},{2,1},{3,2},{4,3},{5,4},{6,5},{7,6},{8,7},{9,8},{10,9},{11,1... | collective-permute-start | bytes 6291464 | tf_op jit(solution)/shard_map/ppermute | solution.py:415
  3.4 68.5 %collective-permute-start = (bf16[64,128,128]{2,1,0:T(8,128)(2,1)}, bf16[64,128,128]{2,1,0:T(8,128)(2,1)}, u32[]{:S(2)}, u32[]{:S(2)}) collective-permute-start(bf16[64,128,128]{2,1,0:T(8,128)(2,1)} %bitcast.24), channel_id=1, source_target_pairs={{0,1},{1,2},{2,3},{3,4},{4,5},{5,6},{6,7},{7,8},{8,9},{9,10},{10,1... | collective-permute-start | bytes 6291464 | tf_op jit(solution)/shard_map/ppermute | solution.py:414
  11.0 3.2 %copy-start.2 = (bf16[8,1024]{1,0:T(8,128)(2,1)S(1)}, bf16[8,1024]{1,0:T(8,128)(2,1)}, u32[]{:S(2)}) copy-start(bf16[8,1024]{1,0:T(8,128)(2,1)} %top.1) | copy-start | bytes 49156
  14.1 1.6 %copy-start.1 = (bf16[8192,128]{1,0:T(8,128)(2,1)S(1)}, bf16[8192,128]{1,0:T(8,128)(2,1)}, u32[]{:S(2)}) copy-start(bf16[8192,128]{1,0:T(8,128)(2,1)} %param.14) | copy-start | bytes 6291460
  62.2 1.3 %copy-start.3 = (bf16[64,128,32]{2,1,0:T(8,128)(2,1)}, bf16[64,128,32]{2,1,0:T(8,128)(2,1)S(1)}, u32[]{:S(2)}) copy-start(bf16[64,128,32]{2,1,0:T(8,128)(2,1)S(1)} %get-tuple-element.13.target) | copy-start | bytes 1572868
  63.5 1.2 %copy-start.4 = (bf16[200,32,128]{2,1,0:T(8,128)(2,1)}, bf16[200,32,128]{2,1,0:T(8,128)(2,1)S(1)}, u32[]{:S(2)}) copy-start(bf16[200,32,128]{2,1,0:T(8,128)(2,1)S(1)} %get-tuple-element.12.source) | copy-start | bytes 4915204
  64.7 1.1 copy-start.6
  69.2 2.7 %copy-start.7 = (bf16[2,16,4,32,128]{4,3,2,1,0:T(8,128)(2,1)S(1)}, bf16[2,16,4,32,128]{4,3,2,1,0:T(8,128)(2,1)}, u32[]{:S(2)}) copy-start(bf16[2,16,4,32,128]{4,3,2,1,0:T(8,128)(2,1)} %copy-done.6) | copy-start | bytes 3145732
  72.0 1.4 %copy-start.5 = (bf16[200,32,128]{2,1,0:T(8,128)(2,1)S(1)}, bf16[200,32,128]{2,1,0:T(8,128)(2,1)}, u32[]{:S(2)}) copy-start(bf16[200,32,128]{2,1,0:T(8,128)(2,1)} %copy-done.4) | copy-start | bytes 4915204

commit v3 on v2

--- a/solution.py
+++ b/solution.py
@@ -15,7 +15,7 @@
 LEAVES = 64
 POOL = 3 * LEAVES
 NNEAR = 27
-PAIRS = (NNEAR + 1) // 2
+HALF = (NNEAR + 1) // 2
 GROUP = 8
 DELTA_SQ = 0.0025
 AXIS = "leaf"
@@ -81,6 +81,7 @@
     tops,
     source,
     target,
+    partner,
     held,
     r_top,
     r_idx,
@@ -126,11 +127,10 @@
         whole.wait_send()
         whole.wait_recv()
 
-    right, left = lax.rem(me + 1, N), lax.rem(me + N - 1, N)
-    to_right = remote(points, others.at[0], 0, right)
-    to_left = remote(points, others.at[1], 1, left)
-    to_right.start()
-    to_left.start()
+    to_partner = remote(points, others.at[0], 0, me + 1 - 2 * core)
+    to_other = remote(points, others.at[1], 1, lax.rem(me - 1 + 2 * core + N, N))
+    to_partner.start()
+    to_other.start()
 
     def give_top(o, c):
         to = lax.rem(plane + o, 16) * GROUP + place
@@ -157,6 +157,8 @@
         copy.start()
 
     fetch.wait()
+    swap = remote(held, partner, 12, me + 1 - 2 * core)
+    swap.start()
 
     def one_mid(m, c):
         rows = []
@@ -218,7 +220,7 @@
         remote(mine, top_all.at[plane], 9, to).start()
     own_top = pltpu.make_async_copy(mine, top_all.at[plane], local.at[0])
     own_top.start()
-    side(features(scale, here, False), put_source(1), LEAVES)
+    side(features(scale, here, False), put_source(0), LEAVES)
     own_top.wait()
 
     finish(r_top.at[pl.ds(0, 15)], 2)
@@ -232,12 +234,12 @@
         remote(part, tops.at[place], 10, to).start()
     own_part = pltpu.make_async_copy(part, tops.at[place], local.at[0])
     own_part.start()
-    to_right.wait()
-    to_left.wait()
-    spare = source[LEAVES]
+    to_partner.wait()
+    to_other.wait()
+    spare = source[0]
     for l in range(8):
         source[POOL + l] = spare
-    side(features(scale, [others[0, i] for i in range(3)], False), put_source(0), LEAVES)
+    side(features(scale, [others[0, i] for i in range(3)], False), put_source(1), LEAVES)
     finish(every.at[0, pl.ds(0, 15)], 8)
     across = remote(every.at[core], every.at[core], 11, me + 1 - 2 * core)
     across.start()
@@ -246,6 +248,7 @@
     own_part.wait()
     finish(tops.at[pl.ds(0, GROUP - 1)], 10)
     across.wait()
+    swap.wait()
     finish(r_blk.at[pl.ds(0, N - 1)], 4)
     finish(r_src.at[pl.ds(0, N - 1)], 5)
 
@@ -263,9 +266,10 @@
             shape((GROUP, 16, K * K), bf16),
             shape((POOL + 8, K, M), bf16),
             shape((LEAVES, M, K), bf16),
+            shape((LEAVES, M, RHS), bf16),
         ),
         in_specs=[inside] * 5 + [pl.BlockSpec(memory_space=pl.ANY)] + [inside] * 4,
-        out_specs=(inside,) * 7,
+        out_specs=(*(inside,) * 7, pl.BlockSpec(memory_space=pl.ANY)),
         scratch_shapes=[
             pltpu.VMEM((LEAVES, M, RHS), bf16),
             pltpu.VMEM((16, 8, K * K), bf16),
@@ -277,25 +281,60 @@
             pltpu.VMEM((16, K * K), bf16),
             pltpu.VMEM((2, 3, LEAVES, M), f32),
             pltpu.VMEM((LEAVES * K, M), f32),
-            pltpu.SemaphoreType.DMA((12,)),
-            pltpu.SemaphoreType.DMA((12,)),
+            pltpu.SemaphoreType.DMA((13,)),
+            pltpu.SemaphoreType.DMA((13,)),
             pltpu.SemaphoreType.DMA((7,)),
         ],
         compiler_params=pltpu.CompilerParams(
-            collective_id=0, has_side_effects=True, vmem_limit_bytes=40 * 1024 * 1024
+            collective_id=0, has_side_effects=True, vmem_limit_bytes=63 * 1024 * 1024
         ),
         cost_estimate=pl.CostEstimate(flops=10**9, bytes_accessed=10**7, transcendentals=0),
         name="exchange",
     )(blk, blk_src, top, top_idx, points, charges, basis, leaf_t, mid_t, base_t)
 
 
+def pair_rows(slot, mine, one, two, j, source, pool, kern, gathered):
+    squares = dot(mine, jnp.concatenate([source[one], source[two]], axis=1))
+    kern[slot, :, 2 * M * j : 2 * M * (j + 1)] = lax.rsqrt(squares.astype(bf16))
+    gathered[slot, 2 * M * j : 2 * M * j + M] = pool[one]
+    gathered[slot, 2 * M * j + M : 2 * M * (j + 1)] = pool[two]
+
+
+def load_pool(refs, pool, sems):
+    copies = [
+        pltpu.make_async_copy(ref, pool.at[pl.ds(LEAVES * i, LEAVES)], sems.at[i])
+        for i, ref in enumerate(refs)
+    ]
+    for copy in copies:
+        copy.start()
+    pool[POOL] = jnp.zeros((M, RHS), bf16)
+    return copies
+
+
+def close_kernel(near, source, target, here, partner, out, pool, kern, gathered, sems):
+    step = pl.program_id(0)
+
+    @pl.when(step == 0)
+    def _():
+        for copy in load_pool((here, partner), pool, sems):
+            copy.wait()
+
+    for b in range(GROUP):
+        first = (step * GROUP + b) * HALF
+        for j in range(HALF // 2):
+            one, two = near[first + 2 * j], near[first + 2 * j + 1]
+            pair_rows(b, target[b], one, two, j, source, pool, kern, gathered)
+        out[b] = dot(kern[b], gathered[b])
+
+
 def near_kernel(
     near,
     source,
     target,
-    before,
     here,
-    after,
+    partner,
+    other,
+    partial,
     a_high,
     a_low,
     every,
@@ -311,54 +350,109 @@
     kern,
     gathered,
     base,
+    extra,
     sems,
 ):
     step = pl.program_id(0)
 
     @pl.when(step == 0)
     def _():
-        copies = [
-            pltpu.make_async_copy(ref, pool.at[pl.ds(LEAVES * i, LEAVES)], sems.at[i])
-            for i, ref in enumerate((before, here, after))
-        ]
-        for copy in copies:
-            copy.start()
-        pool[POOL] = jnp.zeros((M, RHS), bf16)
+        copies = load_pool((here, partner, other), pool, sems)
+        extra[...] = jnp.zeros_like(extra)
         top_field = (dot(t_high[...], top_all[...]) + dot(t_low[...], top_all[...])).astype(bf16)
         coupled = dot(a_high[...], every[...]) + dot(a_low[...], every[...])
         base[...] = (coupled + dot(base_t[...], top_field)).astype(bf16)
         for copy in copies:
             copy.wait()
 
+    late = near[2 * LEAVES * HALF + LEAVES + step]
+
+    @pl.when(late > 0)
+    def _():
+        def one_leaf(b, c):
+            leaf = step * GROUP + b
+
+            def one_entry(e, total):
+                g = near[(LEAVES + leaf) * HALF + e]
+                squares = dot(target[b], source[g])
+                return total + dot(lax.rsqrt(squares.astype(bf16)), pool[g])
+
+            extra[b] = lax.fori_loop(
+                near[2 * LEAVES * HALF + leaf], HALF, one_entry, jnp.zeros((M, RHS), f32)
+            )
+            return c
+
+        lax.fori_loop(0, GROUP, one_leaf, 0)
+
     mid = dot(mid_t[...], base[...]).astype(bf16)
     fields = dot(leaf_t[...], mid).astype(bf16)
     for b in range(GROUP):
-        leaf = step * GROUP + b
-        mine = target[b]
-        for j in range(PAIRS):
-            one = near[leaf * 2 * PAIRS + 2 * j]
-            two = near[leaf * 2 * PAIRS + 2 * j + 1]
-            others = jnp.concatenate([source[one], source[two]], axis=1)
-            squares = dot(mine, others)
-            kern[b, :, 2 * M * j : 2 * M * (j + 1)] = lax.rsqrt(squares.astype(bf16))
-            gathered[b, 2 * M * j : 2 * M * j + M] = pool[one]
-            gathered[b, 2 * M * j + M : 2 * M * (j + 1)] = pool[two]
+        first = (step * GROUP + b) * HALF
+        for j in range(HALF // 2):
+            one, two = near[first + 2 * j], near[first + 2 * j + 1]
+            pair_rows(b, target[b], one, two, j, source, pool, kern, gathered)
         far = dot_t(basis[b], fields[b * K : (b + 1) * K])
-        total = dot(kern[b], gathered[b]) + far
+        total = dot(kern[b], gathered[b]) + far + (partial[b] + extra[b])
         out[pl.ds(b * M, M), :] = total.astype(bf16)
 
-
-def near_call(near, source, target, before, here, after, far, mid_t, leaf_t, basis):
-    count = source.shape[0]
+    @pl.when(late > 0)
+    def _():
+        extra[...] = jnp.zeros_like(extra)
+
+
+def near_scratch():
+    return [
+        pltpu.VMEM((POOL + 1, M, RHS), bf16),
+        pltpu.VMEM((GROUP, M, M * HALF), bf16),
+        pltpu.VMEM((GROUP, M * HALF, RHS), bf16),
+    ]
+
+
+NEAR_PARAMS = dict(
+    compiler_params=pltpu.CompilerParams(
+        vmem_limit_bytes=63 * 1024 * 1024, dimension_semantics=("arbitrary",)
+    ),
+    cost_estimate=pl.CostEstimate(
+        flops=5 * 10**9, bytes_accessed=10**7, transcendentals=10**7
+    ),
+)
+
+
+def close_call(near, source, target, here, partner):
+    anywhere = pl.BlockSpec(memory_space=pl.ANY)
     grid_spec = pltpu.PrefetchScalarGridSpec(
         num_scalar_prefetch=1,
         grid=(LEAVES // GROUP,),
         in_specs=[
-            vmem(count, K, M),
+            vmem(*source.shape),
             pl.BlockSpec((GROUP, M, K), lambda i, _: (i, 0, 0)),
-            pl.BlockSpec(memory_space=pl.ANY),
-            pl.BlockSpec(memory_space=pl.ANY),
-            pl.BlockSpec(memory_space=pl.ANY),
+            anywhere,
+            anywhere,
+        ],
+        out_specs=pl.BlockSpec((GROUP, M, RHS), lambda i, _: (i, 0, 0)),
+        scratch_shapes=[*near_scratch(), pltpu.SemaphoreType.DMA((2,))],
+    )
+    return pl.pallas_call(
+        close_kernel,
+        grid_spec=grid_spec,
+        out_shape=jax.ShapeDtypeStruct((LEAVES, M, RHS), f32),
+        name="close",
+        **NEAR_PARAMS,
+    )(near, source, target, here, partner)
+
+
+def near_call(near, source, target, here, partner, other, partial, far, mid_t, leaf_t, basis):
+    anywhere = pl.BlockSpec(memory_space=pl.ANY)
+    grid_spec = pltpu.PrefetchScalarGridSpec(
+        num_scalar_prefetch=1,
+        grid=(LEAVES // GROUP,),
+        in_specs=[
+            vmem(*source.shape),
+            pl.BlockSpec((GROUP, M, K), lambda i, _: (i, 0, 0)),
+            anywhere,
+            anywhere,
+            anywhere,
+            pl.BlockSpec((GROUP, M, RHS), lambda i, _: (i, 0, 0)),
             *[vmem(*v.shape) for v in far],
             pl.BlockSpec((K, K), lambda i, _: (i, 0)),
             pl.BlockSpec((GROUP * K, K), lambda i, _: (i, 0)),
@@ -366,10 +460,9 @@
         ],
         out_specs=pl.BlockSpec((GROUP * M, RHS), lambda i, _: (i, 0)),
         scratch_shapes=[
-            pltpu.VMEM((POOL + 1, M, RHS), bf16),
-            pltpu.VMEM((GROUP, M, 2 * M * PAIRS), bf16),
-            pltpu.VMEM((GROUP, 2 * M * PAIRS, RHS), bf16),
+            *near_scratch(),
             pltpu.VMEM((K, RHS), bf16),
+            pltpu.VMEM((GROUP, M, RHS), f32),
             pltpu.SemaphoreType.DMA((3,)),
         ],
     )
@@ -377,14 +470,29 @@
         near_kernel,
         grid_spec=grid_spec,
         out_shape=jax.ShapeDtypeStruct((LEAVES * M, RHS), bf16),
-        compiler_params=pltpu.CompilerParams(
-            vmem_limit_bytes=48 * 1024 * 1024, dimension_semantics=("arbitrary",)
-        ),
-        cost_estimate=pl.CostEstimate(
-            flops=10**10, bytes_accessed=10**7, transcendentals=3 * 10**7
-        ),
         name="near",
-    )(near, source, target, before, here, after, *far, mid_t, leaf_t, basis)
+        **NEAR_PARAMS,
+    )(near, source, target, here, partner, other, partial, *far, mid_t, leaf_t, basis)
+
+
+def near_lists(near_leaves, core):
+    block, inside = near_leaves // LEAVES, near_leaves % LEAVES
+    moved = jnp.where(block == 1, 0, jnp.where((block == 0) == (core == 0), 2, 1))
+    place = moved * LEAVES + inside
+    away = place >= 2 * LEAVES
+    column = jnp.arange(NNEAR)
+    key = jnp.where(away, NNEAR, 0) + column
+    rank = jnp.sum(key[:, None, :] < key[:, :, None], axis=2)
+    ordered = jnp.sum(
+        jnp.where(rank[:, :, None] == jnp.arange(2 * HALF), place[:, :, None] + 1, 0), axis=1
+    )
+    ordered = jnp.where(ordered == 0, POOL, ordered - 1)
+    early = ordered[:, :HALF]
+    close = jnp.where(early >= 2 * LEAVES, POOL, early).reshape(-1)
+    ready = jnp.minimum(NNEAR - jnp.sum(away, axis=1), HALF)
+    late = jnp.sum((HALF - ready).reshape(GROUP, GROUP), axis=1)
+    rest = jnp.concatenate([ordered[:, HALF:].reshape(-1), early.reshape(-1), ready, late])
+    return close.astype(jnp.int32), rest.astype(jnp.int32)
 
 
 def high_low(v):
@@ -408,11 +516,7 @@
     top_source,
 ):
     me = lax.axis_index(AXIS)
-    up = [(i, i + 1) for i in range(N - 1)]
-    down = [(i + 1, i) for i in range(N - 1)]
     rows = charges.reshape(LEAVES, M, RHS)
-    before = lax.ppermute(rows, AXIS, up)
-    after = lax.ppermute(rows, AXIS, down)
     points = coords.reshape(3, LEAVES, M)
 
     targets = base_target[:, 0]
@@ -433,9 +537,14 @@
     leaf_t = leaf_transfer.reshape(LEAVES * K, K)
     mid_t = mid_transfer.reshape(GROUP * K, K)
     base_t = base_transfer.reshape(K, K)
-    r_blk, r_src, every, top_all, tops, source, target = exchange_call(
+    r_blk, r_src, every, top_all, tops, source, target, partner = exchange_call(
         blk, blk_src, top_coupling, top_idx, points, rows, basis, leaf_t, mid_t, base_t
     )
+    outward = [(i, i + 1) for i in range(1, N - 1, 2)] + [(i, i - 1) for i in range(2, N, 2)]
+    sent, partner = lax.optimization_barrier((rows, partner))
+    other = lax.ppermute(sent, AXIS, outward)
+    close_list, near_list = near_lists(near_leaves, me % 2)
+    partial = close_call(close_list, source, target, rows, partner)
     by_source = (lane[:, None] == r_src[:, 0, :2].reshape(1, 2 * N)).astype(bf16)
     a = dot(by_source, r_blk.reshape(2 * N, K * K))
     a = a.reshape(N, K, K).transpose(1, 0, 2).reshape(K, N * K)
@@ -448,8 +557,9 @@
         top_all.reshape(16 * K, RHS),
         base_t,
     )
-    near = jnp.pad(near_leaves, ((0, 0), (0, 1)), constant_values=POOL).reshape(-1)
-    return near_call(near, source, target, before, rows, after, far, mid_t, leaf_t, basis)
+    return near_call(
+        near_list, source, target, rows, partner, other, partial, far, mid_t, leaf_t, basis
+    )
 
 
 def solution(mesh):

time: 113 us -> 114 us (level)
  the two profiles are of different devices: /device:TPU:1 before, /device:TPU:32 now
where the time goes in v3:
time: 114 us; the launch traced here: 115 us
  Pallas kernels  84 us (74%)
  local copies, waits for them, and re-layouts  14.5 us (13%)
  other arithmetic  7.7 us (7%)
  starting transfers between devices  7.53 us (7%)
    pallas_call x1, Pallas kernels, exchange_call(): pl.pallas_call(functools.partial(exchange_kernel, math.sqrt(NNEAR * M)),...  32.5 us
    pallas_call x1, Pallas kernels, near_call(): pl.pallas_call(near_kernel, grid_spec=grid_spec, out_shape=jax.ShapeDtype...  29.1 us
    pallas_call x1, Pallas kernels, close_call(): pl.pallas_call(close_kernel, grid_spec=grid_spec, out_shape=jax.ShapeDtyp...  22.4 us
    ppermute x1, starting transfers between devices, per_device(): other = lax.ppermute(sent, AXIS, outward)  7.53 us
    unnamed x20, local copies, waits for them, and re-layouts  2.52 us
  transfers between devices with their start and end apart: 1, of which 0 were waited for; matrix products, arithmetic and copies ran while one was open for 10% of the time, Pallas kernels for 19%

profile of v3, /device:TPU:32, one launch (start us, length us, event | category | flops | bytes accessed | tf_op | source)
XLA Modules:
  0.0 114.8 jit_solution(1062097787966040943)
XLA Ops:
  0.0 1.0 convert_reduce_fusion.2
  1.0 0.7 fusion.12
  1.7 0.1 multiply_reduce_fusion
  1.8 0.7 reduce
  2.6 0.7 reshape.144.base_t
  3.2 0.7 multiply_add_fusion.1
  3.9 0.1 tile.10
  4.0 0.1 sub.66
  4.1 0.7 pad.4.blk_src
  4.8 1.5 %reshape.143.mid_t = bf16[256,32]{1,0:T(8,128)(2,1)} reshape(bf16[8,1024]{1,0:T(8,128)(2,1)} %param.18) | data formatting | bytes 32768 | tf_op jit(solution)/shard_map/reshape | solution.py:538
  6.3 1.5 %copy.36 = f32[1,3,64,128]{3,2,1,0:T(8,128)} copy(f32[1,3,64,128]{3,1,2,0:T(4,128)} %bitcast.35) | data formatting | bytes 196608
  7.8 0.4 convolution_convert_fusion
  8.3 1.0 reshape.138.blk
  9.3 1.1 reshape.142.leaf_t
  10.4 0.9 copy.34
  11.4 0.6 compare_select_fusion.3.top_idx
  12.0 32.5 %exchange.1 = (bf16[128,16,128]{2,1,0:T(8,128)(2,1)}, s32[128,1,128]{2,1,0:T(1,128)}, bf16[2,16,4,32,128]{4,3,2,1,0:T(8,128)(2,1)}, bf16[16,32,128]{2,1,0:T(8,12...) custom-call(bf16[128,16,128]{2,1,0:T(8,128)(2,1)} %reshape.138.blk, ...), custom_call_target="tpu_custom_call" | custom-call | flops 1000000000 | bytes 10000000 | tf_op jit(solution)/shard_map/exchange/pallas_call | solution.py:259
  44.5 7.5 %collective-permute-start = (bf16[64,128,128]{2,1,0:T(8,128)(2,1)}, bf16[64,128,128]{2,1,0:T(8,128)(2,1)}, u32[]{:S(2)}, u32[]{:S(2)}) collective-permute-start(bf16[64,128,128]{2,1,0:T(8,128)(2,1)} %bitcast.22), channel_id=1, source_target_pairs={{1,2},{3,4},{5,6},{7,8},{9,10},{11,12},{13,14},{15,16},{17,18},{19... | collective-permute-start | bytes 6291464 | tf_op jit(solution)/shard_map/ppermute | solution.py:545
  52.1 0.5 broadcast_subtract_fusion
  52.6 0.1 sub.62
  52.7 0.7 reduce_sum.66
  53.4 0.1 convert_reduce_fusion.1
  53.5 0.1 select_reduce_fusion
  53.6 0.1 copy.29
  53.7 0.7 reshape.145.near
  54.4 0.1 copy.27
  54.5 0.7 reshape.137
  55.2 0.1 copy.26
  55.3 0.7 reshape.136
  56.1 1.0 slice_reduce_fusion
  57.1 0.1 eq.116
  57.2 1.0 convert_reduce_fusion
  58.2 0.1 reshape.149
  58.3 0.2 copy.32
  58.5 0.1 reshape.150
  58.6 0.2 reshape.146
  58.9 0.2 copy.30
  59.1 0.3 convolution_bitcast_fusion
  59.4 0.6 copy.31
  60.0 0.0 copy-start.5
  60.0 1.0 reshape.147
  61.0 0.0 copy-done.4
  61.0 0.7 concatenate.3.near
  61.7 0.6 subtract_convert_fusion.1
  62.3 22.4 %close.1.partial = f32[64,128,128]{2,1,0:T(8,128)} custom-call(s32[896]{0:T(1024)} %reshape.145.near, bf16[200,32,128]{2,1,0:T(8,128)(2,1)} %get-tuple-element.15.source, bf16[64,128,32]{2,1,0:T(8,128)(2,1)} %get-tuple-element.16.target, bf16[64,128,128]{2,1,0:T(8,128)(2,1)} %bitcast.23, bf16[64,128,128]{2,1,0:T(8,128)(2,1)} %get-tuple-element.18.partner), custom_call_target="tpu_custom_call" | custom-call | flops 5000000000 | bytes 10000000 | tf_op jit(solution)/shard_map/close/pallas_call | solution.py:435
  84.7 0.8 subtract_convert_fusion
  85.5 0.0 collective-permute-done.other
  85.5 29.1 %near.1 = bf16[8192,128]{1,0:T(8,128)(2,1)} custom-call(s32[1864]{0:T(1024)} %concatenate.3.near, bf16[200,32,128]{2,1,0:T(8,128)(2,1)} %get-tuple-element.15.source, bf16[64,128,32]{2,1,0:T(8,128)(2,1)} %get-tuple-element.16.target, bf16[64,128,128]{2,1,0:T(8,128)(2,1)} %bitcast.24, bf16[64,128,128]{2,1,0:T(8,128)(2,1)} %get-tuple-element.18.partner, ...), custom_call_target="tpu_custom_call" | custom-call | flops 5000000000 | bytes 10000000 | tf_op jit(solution)/shard_map/near/pallas_call | solution.py:469
  (22 shorter events, 0.1 us)
Async XLA Ops:
  0.0 7.8 %copy-start = (bf16[189,1024]{1,0:T(8,128)(2,1)S(1)}, bf16[189,1024]{1,0:T(8,128)(2,1)}, u32[]{:S(2)}) copy-start(bf16[189,1024]{1,0:T(8,128)(2,1)} %param.20) | copy-start | bytes 1161220
  0.0 9.3 %copy-start.3 = (bf16[64,1024]{1,0:T(8,128)(2,1)S(1)}, bf16[64,1024]{1,0:T(8,128)(2,1)}, u32[]{:S(2)}) copy-start(bf16[64,1024]{1,0:T(8,128)(2,1)} %param.17) | copy-start | bytes 393220
  0.0 10.4 %copy-start.1 = (bf16[64,4096]{1,0:T(8,128)(2,1)S(1)}, bf16[64,4096]{1,0:T(8,128)(2,1)}, u32[]{:S(2)}) copy-start(bf16[64,4096]{1,0:T(8,128)(2,1)} %param.16) | copy-start | bytes 1572868
  11.4 40.7 %copy-start.6 = (s32[64,27]{0,1:T(8,128)S(1)}, s32[64,27]{0,1:T(8,128)}, u32[]{:S(2)}) copy-start(s32[64,27]{0,1:T(8,128)} %param.15) | copy-start | bytes 20740
  44.5 14.1 %copy-start.2 = (bf16[128,16,128]{2,1,0:T(8,128)(2,1)S(1)}, bf16[128,16,128]{2,1,0:T(8,128)(2,1)}, u32[]{:S(2)}) copy-start(bf16[128,16,128]{2,1,0:T(8,128)(2,1)} %get-tuple-element.21) | copy-start | bytes 1572868
  44.5 41.0 %collective-permute-start = (bf16[64,128,128]{2,1,0:T(8,128)(2,1)}, bf16[64,128,128]{2,1,0:T(8,128)(2,1)}, u32[]{:S(2)}, u32[]{:S(2)}) collective-permute-start(bf16[64,128,128]{2,1,0:T(8,128)(2,1)} %bitcast.22), channel_id=1, source_target_pairs={{1,2},{3,4},{5,6},{7,8},{9,10},{11,12},{13,14},{15,16},{17,18},{19... | collective-permute-start | bytes 6291464 | tf_op jit(solution)/shard_map/ppermute | solution.py:545
  60.0 1.0 copy-start.4
  60.0 1.0 copy-start.5
  60.0 1.0 copy-start.7
  60.0 1.0 copy-start.8
